TPU v7x, 128 devices: a whole 4x4x4 slice. The times are simulated.
128 devices in a mesh: aa: 8 (over z, core), ba: 4 (over y), col: 4 (over x).
Axes of the slice: x: 4, y: 4, z: 4, core: 2. Of those that a mesh axis runs over, the one named last changes fastest.
Arguments:
- tokens: bfloat16 [4096, 7168], P(('aa', 'col'), 'ba'), may hold values from -6 to 6
- routing: int32 [4096, 8], P(('aa', 'col')), may hold values from 0 to 31, all different within a row; in each aligned block of 128 rows (0 to 127, 128 to 255, ...) at most 40 rows name the same one
- gate_codes: int32 [4096, 8], P(('aa', 'col')), may hold values from 1 to 65535
- w_gate: bfloat16 [32, 7168, 2048], P(('aa', 'col'), None, 'ba'), may hold values from -0.0625 to 0.0625
- w_up: bfloat16 [32, 7168, 2048], P(('aa', 'col'), None, 'ba'), may hold values from -0.0625 to 0.0625
- w_down: bfloat16 [32, 2048, 7168], P(('aa', 'col'), 'ba'), may hold values from -0.125 to 0.125
Outputs:
- mixed: bfloat16 [4096, 7168], P(('aa', 'col'), 'ba')
Inputs may be any that keep to these rules, and one draw needn't show every extreme that they name: `routing`: within each token group of 128 rows (aligned blocks of the rows), no expert is named more than 40 times, a bound that some block reaches. A token names 8 different experts.
All inputs are finite; a program needn't handle non-finite values.
Results may differ from a plain program's by a relative error of at most 0.014.
Values may be sent and summed in bfloat16 or wider, within the bound.
A program may use at most 192 MiB of HBM per device.

v0:
```python
import jax
import jax.numpy as jnp
from jax import lax
from jax.sharding import PartitionSpec as P

route_scale = 2.827


def route_tables(routing, experts, slots_each, top):
    flat = routing.reshape(-1)
    onehot = (flat[:, None] == jnp.arange(experts, dtype=jnp.int32)[None, :]).astype(jnp.int32)
    before = jnp.cumsum(onehot, axis=0) - onehot
    pos = jnp.sum(before * onehot, axis=1)
    slot = flat * slots_each + pos
    matched = slot[:, None] == jnp.arange(experts * slots_each, dtype=jnp.int32)[None, :]
    owner = jnp.arange(flat.shape[0], dtype=jnp.int32) // top
    slot_token = jnp.sum(jnp.where(matched, owner[:, None], 0), axis=0)
    live = jnp.any(matched, axis=0)
    return (slot, slot_token.reshape(experts, slots_each), live.reshape(experts, slots_each))


def on_device(tokens, routing, gate_codes, w_gate, w_up, w_down):
    n_aa = lax.axis_size("aa")
    n_col = lax.axis_size("col")
    experts = n_aa * n_col
    tok_rows = tokens.shape[0]
    top = routing.shape[1]
    slots_each = min(tok_rows, 5 * tok_rows * top // (4 * experts))
    slot, slot_token, live = route_tables(routing, experts, slots_each, top)
    codes = gate_codes.astype(jnp.float32)
    weight = route_scale * codes / jnp.sum(codes, axis=1, keepdims=True)
    outgoing = jnp.where(live[:, :, None], tokens[slot_token], jnp.zeros((), jnp.bfloat16))
    gate_local = w_gate[0]
    up_local = w_up[0]
    down_local = w_down[0]
    full_rows = lax.all_gather(
        lax.all_to_all(outgoing, ("aa", "col"), split_axis=0, concat_axis=0, tiled=True),
        "ba",
        axis=2,
        tiled=True,
    )
    sources = full_rows.shape[0]
    count = full_rows.shape[1]
    rows = full_rows.reshape(sources * count, full_rows.shape[2])
    gate = jnp.dot(rows, gate_local, preferred_element_type=jnp.float32)
    upper = jnp.dot(rows, up_local, preferred_element_type=jnp.float32)
    hidden = (jax.nn.silu(gate) * upper).astype(jnp.bfloat16)
    partial_out = jnp.dot(hidden, down_local, preferred_element_type=jnp.float32).astype(
        jnp.bfloat16
    )
    summed = lax.psum_scatter(partial_out, "ba", scatter_dimension=1, tiled=True).astype(
        jnp.float32
    )
    returned = lax.all_to_all(
        summed.astype(jnp.bfloat16).reshape(sources, count, summed.shape[1]),
        ("aa", "col"),
        split_axis=0,
        concat_axis=0,
        tiled=True,
    )
    table = returned.reshape(experts * slots_each, returned.shape[2])
    picked = table[slot].reshape(tok_rows, top, table.shape[1]).astype(jnp.float32)
    mixed = jnp.einsum("tk,tkd->td", weight, picked)
    return mixed.astype(jnp.bfloat16)


def solution(mesh):
    return jax.shard_map(
        on_device,
        mesh=mesh,
        in_specs=(
            P(("aa", "col"), "ba"),
            P(("aa", "col"), None),
            P(("aa", "col"), None),
            P(("aa", "col"), None, "ba"),
            P(("aa", "col"), None, "ba"),
            P(("aa", "col"), "ba", None),
        ),
        out_specs=P(("aa", "col"), "ba"),
        check_vma=False,
    )
```

profile of v0, /device:TPU:0, one launch (start us, length us, event | category | flops | bytes accessed | tf_op | source)
XLA Modules:
  0.0 548.4 jit_solution(2323439232883052504)
XLA Ops:
  6.5 0.8 copy.12
  7.4 0.1 eq.39
  7.5 0.1 reshape.111
  7.6 9.0 %reduce-window.6 = s32[32,8,128]{2,1,0:T(8,128)S(1)} reduce-window(s32[32,8,128]{2,1,0:T(8,128)S(1)} %fusion.17, s32[]{:T(128)} %constant.32.clone.1), window={size=1x1x128 pad=0_0x0_0x127_0}, to_apply=%region_1.2 | reduce-window | flops 4161536 | bytes 262148 | tf_op jit(solution)/shard_map/reduce-window
  16.6 0.1 slice.12
  16.7 0.1 copy.14
  16.9 0.1 copy.15
  16.9 0.1 broadcast_add_fusion
  17.1 0.8 fusion.5
  17.9 0.7 select_reduce_fusion
  18.6 0.1 reshape.113
  18.7 0.1 reshape.120
  18.8 0.1 broadcast_in_dim.33
  18.9 5.8 %gather_fusion = bf16[1280,1792]{1,0:T(8,128)(2,1)} fusion(bf16[128,1792]{1,0:T(8,128)(2,1)S(1)} %copy-done, s32[2048]{0:T(1024)S(1)} %pad_clamp_fusion), kind=kCustom, calls=%fused_computation | custom fusion | bytes 9180160 | tf_op jit(solution)/shard_map/gather | solution.py:32
  24.7 2.7 broadcast_select_fusion
  27.4 63.4 %all_to_all.10 = bf16[32,40,1792]{2,1,0:T(8,128)(2,1)} all-to-all(bf16[32,40,1792]{2,1,0:T(8,128)(2,1)S(1)} %broadcast_select_fusion), channel_id=1, replica_groups=mesh['aa'=8,'ba'=4,'col'=4] {'aa','col'}, dimensions={0} | all-to-all | bytes 9175040 | tf_op jit(solution)/shard_map/all_to_all | solution.py:37
  90.8 0.0 all-gather.2.cloned.1.call-update
  90.9 0.2 reduce-scatter.2.cloned.1.call-start
  91.1 166.3 %all-gather.2.cloned.1.call-done = bf16[32,40,7168]{2,1,0:T(8,128)(2,1)} async-done(((bf16[32,40,1792]{2,1,0:T(8,128)(2,1)}), bf16[32,40,7168]{2,1,0:T(8,128)(2,1)}) %all-gather.2.cloned.1.call-update) | async-done | bytes 18350096 | tf_op jit(solution)/shard_map/all_gather | solution.py:36
  257.4 16.7 %fusion.3 = f32[1280,512]{1,0:T(8,128)} fusion(bf16[1280,7168]{1,0:T(8,128)(2,1)} %bitcast.57, bf16[1,7168,512]{2,1,0:T(8,128)(2,1)} %param.9), kind=kOutput, calls=%fused_computation.6 | convolution fusion | flops 9395240960 | bytes 28311552 | tf_op jit(solution)/shard_map/dot_general | solution.py:45
  274.1 13.1 %fusion.11 = bf16[1280,512]{1,0:T(8,128)(2,1)S(1)} fusion(bf16[1280,7168]{1,0:T(8,128)(2,1)S(1)} %bitcast.58, bf16[1,7168,512]{2,1,0:T(8,128)(2,1)} %param.10, f32[1280,512]{1,0:T(8,128)} %fusion.3), kind=kOutput, calls=%fused_computation.15 | convolution fusion | flops 9399173120 | bytes 29622272 | tf_op jit(solution)/shard_map/dot_general | solution.py:46
  287.2 16.1 %convolution_convert_fusion = bf16[1280,7168]{1,0:T(8,128)(2,1)} fusion(bf16[1280,512]{1,0:T(8,128)(2,1)S(1)} %fusion.11, bf16[1,512,7168]{2,1,0:T(8,128)(2,1)} %param.11), kind=kOutput, calls=%fused_computation.2 | convolution fusion | flops 9404416000 | bytes 27000832 | tf_op jit(solution)/shard_map/dot_general | solution.py:48
  303.3 0.0 reduce-scatter.2.cloned.1.call-update
  303.3 160.7 %reduce-scatter.2.cloned.1.call-done = bf16[1280,1792]{1,0:T(8,128)(2,1)} async-done(((bf16[1280,7168]{1,0:T(8,128)(2,1)}), bf16[1280,1792]{1,0:T(8,128)(2,1)}) %reduce-scatter.2.cloned.1.call-update) | async-done | bytes 4587536 | tf_op jit(solution)/shard_map/reduce_scatter | solution.py:51
  464.0 7.7 %all-to-all-start.1 = ((bf16[32,40,1792]{2,1,0:T(8,128)(2,1)}), bf16[32,40,1792]{2,1,0:T(8,128)(2,1)}, u32[]{:S(2)}, u32[]{:S(2)}) async-start(bf16[32,40,1792]{2,1,0:T(8,128)(2,1)} %bitcast.52), calls=%async_computation.2 | async-start | bytes 9175040 | tf_op jit(solution)/shard_map/all_to_all | solution.py:54
  471.7 0.1 copy.16
  471.8 0.1 mul.48
  472.0 0.1 copy.17
  472.1 54.6 %all-to-all-done.1 = bf16[32,40,1792]{2,1,0:T(8,128)(2,1)} async-done(((bf16[32,40,1792]{2,1,0:T(8,128)(2,1)}), bf16[32,40,1792]{2,1,0:T(8,128)(2,1)}, u32[]{:S(2)}, u32[]{:S(2)}) %all-to-all-start.1) | async-done | bytes 4587552 | tf_op jit(solution)/shard_map/all_to_all | solution.py:54
  526.7 10.9 %gather_fusion.1 = bf16[1024,1792]{1,0:T(8,128)(2,1)} fusion(bf16[1280,1792]{1,0:T(8,128)(2,1)} %bitcast.9, s32[1024]{0:T(1024)S(1)} %broadcast_clamp_fusion), kind=kCustom, calls=%fused_computation.1 | custom fusion | bytes 7344128 | tf_op jit(solution)/shard_map/gather | solution.py:62
  537.6 3.1 fusion.9
  540.7 0.8 copy.22
  (23 shorter events, 0.2 us)
Async XLA Ops:
  6.5 12.3 %copy-start = (bf16[128,1792]{1,0:T(8,128)(2,1)S(1)}, bf16[128,1792]{1,0:T(8,128)(2,1)}, u32[]{:S(2)}) copy-start(bf16[128,1792]{1,0:T(8,128)(2,1)} %param.6) | copy-start | bytes 1376260
  6.5 250.9 %all-gather.2.cloned.1.call-start = ((), (), s32[]{:S(2)}) async-start(), calls=%async_computation.3 | async-start | bytes 22937600 | tf_op jit(solution)/shard_map/all_gather | solution.py:36
  90.9 373.2 %reduce-scatter.2.cloned.1.call-start = ((), (), s32[]{:S(2)}) async-start(), calls=%async_computation.4 | async-start | bytes 22937600 | tf_op jit(solution)/shard_map/reduce_scatter | solution.py:51
  257.4 16.7 %copy-start.4 = (bf16[32,40,7168]{2,1,0:T(8,128)(2,1)S(1)}, bf16[32,40,7168]{2,1,0:T(8,128)(2,1)}, u32[]{:S(2)}) copy-start(bf16[32,40,7168]{2,1,0:T(8,128)(2,1)} %all-gather.2.cloned.1.call-done) | copy-start | bytes 55050244
  464.0 7.7 %copy-start.2 = (s32[128,8]{0,1:T(8,128)S(1)}, s32[128,8]{0,1:T(8,128)}, u32[]{:S(2)}) copy-start(s32[128,8]{0,1:T(8,128)} %param.7) | copy-start | bytes 12292
  464.0 7.9 %copy-start.3 = (s32[128,8]{0,1:T(8,128)S(1)}, s32[128,8]{0,1:T(8,128)}, u32[]{:S(2)}) copy-start(s32[128,8]{0,1:T(8,128)} %param.8) | copy-start | bytes 12292
  464.0 62.7 %all-to-all-start.1 = ((bf16[32,40,1792]{2,1,0:T(8,128)(2,1)}), bf16[32,40,1792]{2,1,0:T(8,128)(2,1)}, u32[]{:S(2)}, u32[]{:S(2)}) async-start(bf16[32,40,1792]{2,1,0:T(8,128)(2,1)} %bitcast.52), calls=%async_computation.2 | async-start | bytes 9175040 | tf_op jit(solution)/shard_map/all_to_all | solution.py:54
  526.7 14.8 %copy-start.1 = (bf16[128,1792]{1,0:T(8,128)(2,1)S(1)}, bf16[128,1792]{1,0:T(8,128)(2,1)}, u32[]{:S(2)}) copy-start(bf16[128,1792]{1,0:T(8,128)(2,1)} %param.6) | copy-start | bytes 1376260
Sparse Core Ops, SparseCore 0:
  91.0 166.3 all-gather.1
  303.4 160.5 reduce-scatter.1
where the time goes:
time: 550 us; the launch traced here: 548 us
  waiting for transfers between devices  382 us (69%)
  blocking collectives  63.4 us (12%)
  matrix products  49 us (9%)
  local copies, waits for them, and re-layouts  19.4 us (4%)
  between operations  13.6 us (2%)
  other arithmetic  13.4 us (2%)
  starting transfers between devices  7.9 us (1%)
    all_gather x1, waiting for transfers between devices, on_device(): lax.all_gather(lax.all_to_all(outgoing, ('aa', 'col'), split_axis=0, conc...  166 us
    reduce_scatter x1, waiting for transfers between devices, on_device(): lax.psum_scatter(partial_out, 'ba', scatter_dimension=1, tiled=True)  161 us
    all_to_all x1, blocking collectives, on_device(): lax.all_to_all(outgoing, ('aa', 'col'), split_axis=0, concat_axis=0, tile...  63.4 us
    all_to_all x1, waiting for transfers between devices, on_device(): lax.all_to_all(summed.astype(jnp.bfloat16).reshape(sources, count, summed...  54.6 us
    dot_general x1, matrix products, on_device(): gate = jnp.dot(rows, gate_local, preferred_element_type=jnp.float32)  16.7 us
    dot_general x1, matrix products, on_device(): jnp.dot(hidden, down_local, preferred_element_type=jnp.float32)  16.1 us
    dot_general x1, matrix products, on_device(): upper = jnp.dot(rows, up_local, preferred_element_type=jnp.float32)  13.1 us
  transfers between devices with their start and end apart: 3, of which 3 were waited for; matrix products, arithmetic and copies ran while one was open for 0% of the time, Pallas kernels for 0%

commit v1 on v0

v1 whole, which is shorter than its diff:
```python
import functools
import jax
import jax.numpy as jnp
from jax import lax
from jax.experimental import pallas as pl
from jax.experimental.pallas import tpu as pltpu
from jax.sharding import PartitionSpec as P

MESH = pl.DeviceIdType.MESH
route_scale = 2.827
bf16 = jnp.bfloat16
f32 = jnp.float32
TILE = 128
ORDERS = (("x", "y", "z"), ("y", "z", "x"), ("z", "x", "y"))


def route_tables(routing, experts, slots_each, top):
    flat = routing.reshape(-1)
    onehot = (flat[:, None] == jnp.arange(experts, dtype=jnp.int32)[None, :]).astype(jnp.int32)
    before = jnp.cumsum(onehot, axis=0) - onehot
    pos = jnp.sum(before * onehot, axis=1)
    slot = flat * slots_each + pos
    matched = slot[:, None] == jnp.arange(experts * slots_each, dtype=jnp.int32)[None, :]
    owner = jnp.arange(flat.shape[0], dtype=jnp.int32) // top
    slot_token = jnp.sum(jnp.where(matched, owner[:, None], 0), axis=0)
    live = jnp.any(matched, axis=0)
    return (slot, slot_token.reshape(experts, slots_each), live.reshape(experts, slots_each))


def place():
    aa = lax.axis_index("aa")
    z, core = aa // 2, aa % 2
    return {"z": z, "y": lax.axis_index("ba"), "x": lax.axis_index("col")}, core


def peer(me, core, axis, step):
    at = lax.rem(me[axis] + (step + 4), 4)
    if axis == "z":
        return {"aa": at * 2 + core}
    return {"ba": at} if axis == "y" else {"col": at}


def greet(me, core):
    barrier = pltpu.get_barrier_semaphore()
    for axis in "xyz":
        for step in (1, -1):
            pl.semaphore_signal(barrier, inc=1, device_id=peer(me, core, axis, step), device_id_type=MESH)
    pl.semaphore_signal(barrier, inc=1, device_id={"aa": me["z"] * 2 + (1 - core)}, device_id_type=MESH)
    pl.semaphore_wait(barrier, 7)


def combine_kernel(slots, own_ref, other_ref, down_ref, spread_ref, out_ref,
                   send_rows, pair_rows, in1, in2, in3, got1, got2, got3, more1, more2, more3,
                   send_sem, recv_sem, pair_send, pair_recv, credit):
    me, core = place()
    partner = {"aa": me["z"] * 2 + (1 - core)}
    ins, gots, mores = (in1, in2, in3), (got1, got2, got3), (more1, more2, more3)
    quarter = out_ref.shape[1]
    greet(me, core)

    def ring(r, phase, slot, kind):
        p = lax.rem(slot, 2)
        buf = ins[phase].at[r, p]
        b = ins[phase].shape[2] // 4
        h = b // 2
        axis = ORDERS[r][phase]
        src, dst, step = (
            (buf.at[pl.ds(b + h, b)], gots[phase].at[r, p, 0], 1),
            (buf.at[pl.ds(2 * b + h, b)], gots[phase].at[r, p, 1], -1),
            (buf.at[pl.ds(b, h)], mores[phase].at[r, p, 0], 1),
            (buf.at[pl.ds(3 * b + h, h)], mores[phase].at[r, p, 1], -1),
        )[kind]
        return pltpu.make_async_remote_copy(
            src_ref=src, dst_ref=dst, send_sem=send_sem.at[r, phase, kind, p], recv_sem=recv_sem.at[r, phase, kind, p],
            device_id=peer(me, core, axis, step), device_id_type=MESH)

    def pair(r, slot):
        p = lax.rem(slot, 2)
        return pltpu.make_async_remote_copy(
            src_ref=send_rows.at[r], dst_ref=pair_rows.at[r, p, :, pl.ds(80, 80)], send_sem=pair_send.at[r],
            recv_sem=pair_recv.at[r, p], device_id=partner, device_id_type=MESH)

    def tiles(rows, body):
        size = min(rows, 256)
        if rows == size:
            body(0, size)
        else:
            @pl.loop(0, rows // size)
            def _(i):
                body(pl.multiple_of(i * size, size), size)

    def project(r, slot):
        p = lax.rem(slot, 2)
        first = (slot * 3 + r) * TILE
        w = jnp.concatenate(
            [down_ref[:, pl.ds(pl.multiple_of(q * quarter + first, TILE), TILE)] for q in range(4)], axis=1)
        pair_rows[r, p, :, 0:80, :] = jnp.dot(own_ref[...], w, preferred_element_type=f32).astype(bf16).reshape(8, 80, 4 * TILE)

        @pl.when(slot >= 1)
        def _():
            pair(r, slot - 1).wait_send()

        send_rows[r] = jnp.dot(other_ref[...], w, preferred_element_type=f32).astype(bf16).reshape(8, 80, 4 * TILE)
        pair(r, slot).start()

        @pl.when(slot == slots[r] - 1)
        def _():
            pair(r, slot).wait_send()

    def begin(r, phase, slot):
        @pl.when(slot >= 2)
        def _():
            pl.semaphore_wait(credit.at[r, phase, 0], 1)
            pl.semaphore_wait(credit.at[r, phase, 1], 1)

        ring(r, phase, slot, 0).start()
        ring(r, phase, slot, 1).start()

    def scatter(r, slot):
        p = lax.rem(slot, 2)
        pair(r, slot).wait_recv()
        weight = {axis: 4 ** (2 - ORDERS[r].index(axis)) for axis in "xyz"}

        @pl.loop(0, 8)
        def _(n):
            z = n // 2
            rows = jnp.dot(spread_ref[n], pair_rows[r, p, n], preferred_element_type=f32).astype(bf16)
            to_z = lax.rem(z - me["z"] + 4, 4) * weight["z"]
            for half in range(2):
                x = lax.rem(n, 2) * 2 + half
                to_zx = to_z + lax.rem(x - me["x"] + 4, 4) * weight["x"]
                for q in range(4):
                    at = to_zx + lax.rem(q - me["y"] + 4, 4) * weight["y"]
                    in1[r, p, pl.ds(pl.multiple_of(at * 128, 128), 128), :] = rows[half * 128:half * 128 + 128, q * TILE:(q + 1) * TILE]
        begin(r, 0, slot)

    def middle(r, phase, slot):
        p = lax.rem(slot, 2)
        buf, got = ins[phase], gots[phase]
        b = buf.shape[2] // 4
        h = b // 2
        ring(r, phase, slot, 0).wait_recv()

        def right(i, n):
            a = buf[r, p, pl.ds(b + i, n), :].astype(f32) + got[r, p, 0, pl.ds(h + i, n), :].astype(f32)
            buf[r, p, pl.ds(b + i, n), :] = a.astype(bf16)
        tiles(h, right)
        ring(r, phase, slot, 2).start()
        ring(r, phase, slot, 1).wait_recv()

        def left(i, n):
            a = buf[r, p, pl.ds(3 * b + h + i, n), :].astype(f32) + got[r, p, 1, pl.ds(i, n), :].astype(f32)
            buf[r, p, pl.ds(3 * b + h + i, n), :] = a.astype(bf16)
        tiles(h, left)
        ring(r, phase, slot, 3).start()

    def finish(r, phase, slot):
        p = lax.rem(slot, 2)
        buf, got, more = ins[phase], gots[phase], mores[phase]
        b = buf.shape[2] // 4
        h = b // 2
        ring(r, phase, slot, 2).wait_recv()
        ring(r, phase, slot, 3).wait_recv()

        def put(at, n, value):
            if phase < 2:
                ins[phase + 1][r, p, pl.ds(at, n), :] = value.astype(bf16)
            else:
                col = pl.multiple_of((slot * 3 + r) * TILE, TILE)
                out_ref[pl.ds(at, n), pl.ds(col, TILE)] = value.astype(bf16)

        def first(i, n):
            put(i, n, buf[r, p, pl.ds(i, n), :].astype(f32) + got[r, p, 1, pl.ds(h + i, n), :].astype(f32)
                + more[r, p, 0, pl.ds(i, n), :].astype(f32))
        tiles(h, first)

        def second(i, n):
            put(h + i, n, buf[r, p, pl.ds(h + i, n), :].astype(f32) + got[r, p, 0, pl.ds(i, n), :].astype(f32)
                + more[r, p, 1, pl.ds(i, n), :].astype(f32))
        tiles(h, second)
        for kind in range(4):
            ring(r, phase, slot, kind).wait_send()

        @pl.when(slot + 2 < slots[r])
        def _():
            axis = ORDERS[r][phase]
            pl.semaphore_signal(credit.at[r, phase, 0], inc=1, device_id=peer(me, core, axis, 1), device_id_type=MESH)
            pl.semaphore_signal(credit.at[r, phase, 1], inc=1, device_id=peer(me, core, axis, -1), device_id_type=MESH)

        if phase < 2:
            begin(r, phase + 1, slot)

    def stage(step, delay, body):
        for r in range(3):
            slot = step - delay

            @pl.when((slot >= 0) & (slot < slots[r]))
            def _():
                body(r, slot)

    @pl.loop(0, max(slots) + 7)
    def _(step):
        stage(step, 2, lambda r, s: middle(r, 0, s))
        stage(step, 4, lambda r, s: middle(r, 1, s))
        stage(step, 6, lambda r, s: middle(r, 2, s))
        stage(step, 7, lambda r, s: finish(r, 2, s))
        stage(step, 5, lambda r, s: finish(r, 1, s))
        stage(step, 3, lambda r, s: finish(r, 0, s))
        stage(step, 1, scatter)
        stage(step, 0, project)


def combine(own, other, down, spread):
    quarter = down.shape[1] // 4
    count = quarter // TILE
    slots = tuple((count - r + 2) // 3 for r in range(3))
    vmem = pl.BlockSpec(memory_space=pltpu.VMEM)

    def buffers(parts, rows):
        return pltpu.VMEM((3, 2) + parts + (rows, TILE), bf16)

    return pl.pallas_call(
        functools.partial(combine_kernel, slots),
        out_shape=jax.ShapeDtypeStruct((128, quarter), bf16),
        in_specs=[vmem] * 4,
        out_specs=vmem,
        scratch_shapes=[
            pltpu.VMEM((3, 8, 80, 4 * TILE), bf16),
            pltpu.VMEM((3, 2, 8, 160, 4 * TILE), bf16),
            buffers((), 8192), buffers((), 2048), buffers((), 512),
            buffers((2,), 2048), buffers((2,), 512), buffers((2,), 128),
            buffers((2,), 1024), buffers((2,), 256), buffers((2,), 64),
            pltpu.SemaphoreType.DMA((3, 3, 4, 2)),
            pltpu.SemaphoreType.DMA((3, 3, 4, 2)),
            pltpu.SemaphoreType.DMA((3,)),
            pltpu.SemaphoreType.DMA((3, 2)),
            pltpu.SemaphoreType.REGULAR((3, 3, 2)),
        ],
        compiler_params=pltpu.CompilerParams(collective_id=1, has_side_effects=True, vmem_limit_bytes=66000000),
        name="combine",
    )(own, other, down, spread)


def expert_tables(routing, weight, expert, cap):
    named = routing == expert
    taken = jnp.any(named, axis=2)
    ones = taken.astype(f32)
    rank = jnp.arange(128)
    pos = jnp.dot(ones, (rank[:, None] < rank[None, :]).astype(f32)).astype(jnp.int32)
    hot = taken[:, :, None] & (pos[:, :, None] == jnp.arange(cap, dtype=jnp.int32)[None, None, :])
    gain = jnp.sum(jnp.where(named, weight, 0.0), axis=2)
    return hot, jnp.sum(jnp.where(hot, gain[:, :, None], 0.0), axis=1)


def spread_matrix(hot_own, hot_other, core):
    def mine(hot):
        by = hot.reshape(4, 2, 2, 2, 128, 40)
        return lax.dynamic_index_in_dim(by, core, 1, keepdims=False)
    both = jnp.stack([mine(hot_own), mine(hot_other)], axis=4)
    eye = jnp.eye(2, dtype=bool)
    wide = both[:, :, :, :, :, None, :] & eye[None, None, :, None, None, :, None]
    return wide.reshape(8, 256, 160).astype(bf16)


def on_device(tokens, routing, gate_codes, w_gate, w_up, w_down):
    experts = lax.axis_size("aa") * lax.axis_size("col")
    tok_rows = tokens.shape[0]
    top = routing.shape[1]
    cap = min(tok_rows, 5 * tok_rows * top // (4 * experts))
    aa, col = lax.axis_index("aa"), lax.axis_index("col")
    core = aa % 2
    slot, slot_token, live = route_tables(routing, experts, cap, top)
    all_codes = lax.all_gather(jnp.concatenate([routing, gate_codes], axis=1), ("aa", "col"), axis=0, tiled=False)
    all_routing = all_codes[:, :, :top]
    codes = all_codes[:, :, top:].astype(f32)
    weight = route_scale * codes / jnp.sum(codes, axis=2, keepdims=True)
    hot_own, gain_own = expert_tables(all_routing, weight, aa * 4 + col, cap)
    hot_other, _ = expert_tables(all_routing, weight, (aa + 1 - 2 * core) * 4 + col, cap)
    spread = spread_matrix(hot_own, hot_other, core)
    outgoing = jnp.where(live[:, :, None], tokens[slot_token], jnp.zeros((), bf16))
    full_rows = lax.all_gather(
        lax.all_to_all(outgoing, ("aa", "col"), split_axis=0, concat_axis=0, tiled=True),
        "ba",
        axis=2,
        tiled=True,
    )
    rows = full_rows.reshape(experts * cap, full_rows.shape[2])
    gate = jnp.dot(rows, w_gate[0], preferred_element_type=f32)
    upper = jnp.dot(rows, w_up[0], preferred_element_type=f32)
    hidden = (jax.nn.silu(gate) * upper * gain_own.reshape(-1, 1)).astype(bf16)
    by_core = hidden.reshape(4, 2, 160, hidden.shape[1])
    own = lax.dynamic_index_in_dim(by_core, core, 1, keepdims=False).reshape(640, -1)
    other = lax.dynamic_index_in_dim(by_core, 1 - core, 1, keepdims=False).reshape(640, -1)
    return combine(own, other, w_down[0], spread)


def solution(mesh):
    return jax.shard_map(
        on_device,
        mesh=mesh,
        in_specs=(
            P(("aa", "col"), "ba"),
            P(("aa", "col"), None),
            P(("aa", "col"), None),
            P(("aa", "col"), None, "ba"),
            P(("aa", "col"), None, "ba"),
            P(("aa", "col"), "ba", None),
        ),
        out_specs=P(("aa", "col"), "ba"),
        check_vma=False,
    )
```

time: 550 us -> 446 us (0.81)
  waiting for transfers between devices: 382 us -> 122 us
  Pallas kernels: 0 us -> 148 us
  blocking collectives: 63.4 us -> 102 us
  matrix products: 49 us -> 30.8 us
  starting transfers between devices: 7.9 us -> 0.01 us
    reduce_scatter x1 -> x0, waiting for transfers between devices: 161 us -> none  [on_device(): lax.psum_scatter(partial_out, 'ba', scatter_dimension=1, tiled=True)]
    pallas_call x0 -> x1, Pallas kernels: none -> 148 us  [combine(): pl.pallas_call(functools.partial(combine_kernel, slots), out_shape=jax.Sh...]
    all_to_all x1 -> x0, waiting for transfers between devices: 54.6 us -> none  [on_device(): lax.all_to_all(summed.astype(jnp.bfloat16).reshape(sources, count, summed...]
    all_gather x1, waiting for transfers between devices: 166 us -> 122 us  [on_device(): lax.all_gather(lax.all_to_all(outgoing, ('aa', 'col'), split_axis=0, conc...]
    all_gather x0 -> x1, blocking collectives: none -> 38.2 us  [on_device(): lax.all_gather(jnp.concatenate([routing, gate_codes], axis=1), ('aa', 'co...]
    dot_general x4, matrix products: 49 us -> 30.8 us  [the longest x1 15.9 us: on_device(): upper = jnp.dot(rows, w_up[0], preferred_element_type=f32)]
    gather x1 -> x0, local copies, waits for them, and re-layouts: 10.9 us -> none  [on_device(): table[slot].reshape(tok_rows, top, table.shape[1]).astype(jnp.float32)]
    all_to_all x1 -> x0, starting transfers between devices: 7.68 us -> none  [on_device(): lax.all_to_all(summed.astype(jnp.bfloat16).reshape(sources, count, summed...]
  transfers between devices with their start and end apart: 3 -> 1, of which waited for: 3 -> 1; matrix products, arithmetic and copies ran while one was open for 0% -> 1% of each run, Pallas kernels for 0% -> 0%
where the time goes in v1:
time: 446 us
  Pallas kernels  148 us (33%)
  waiting for transfers between devices  122 us (27%)
  blocking collectives  102 us (23%)
  matrix products  30.8 us (7%)
  other arithmetic  15.1 us (3%)
  local copies, waits for them, and re-layouts  14.4 us (3%)
  between operations  13.7 us (3%)
    pallas_call x1, Pallas kernels, combine(): pl.pallas_call(functools.partial(combine_kernel, slots), out_shape=jax.Sh...  148 us
    all_gather x1, waiting for transfers between devices, on_device(): lax.all_gather(lax.all_to_all(outgoing, ('aa', 'col'), split_axis=0, conc...  122 us
    all_to_all x1, blocking collectives, on_device(): lax.all_to_all(outgoing, ('aa', 'col'), split_axis=0, concat_axis=0, tile...  63.4 us
    all_gather x1, blocking collectives, on_device(): lax.all_gather(jnp.concatenate([routing, gate_codes], axis=1), ('aa', 'co...  38.2 us
    dot_general x1, matrix products, on_device(): upper = jnp.dot(rows, w_up[0], preferred_element_type=f32)  15.9 us
    dot_general x1, matrix products, on_device(): gate = jnp.dot(rows, w_gate[0], preferred_element_type=f32)  14.6 us
    another operation x3, other arithmetic  9.15 us
  transfers between devices with their start and end apart: 1, of which 1 were waited for; matrix products, arithmetic and copies ran while one was open for 1% of the time, Pallas kernels for 0%

profile of v1, /device:TPU:0, one launch (start us, length us, event | category | flops | bytes accessed | tf_op | source)
XLA Modules:
  0.0 445.7 jit_solution(14028207854093691309)
XLA Ops:
  6.5 0.8 copy.20
  7.4 0.1 eq.98
  7.5 0.1 reshape.116
  7.6 9.0 %reduce-window.6 = s32[32,8,128]{2,1,0:T(8,128)S(1)} reduce-window(s32[32,8,128]{2,1,0:T(8,128)S(1)} %fusion.22, s32[]{:T(128)} %constant.60.clone.1), window={size=1x1x128 pad=0_0x0_0x127_0}, to_apply=%region_0.1 | reduce-window | flops 4161536 | bytes 262148 | tf_op jit(solution)/shard_map/reduce-window
  16.6 0.1 slice.18
  16.7 0.1 copy.22
  16.9 0.1 broadcast_add_fusion
  17.1 0.8 fusion.4
  17.9 0.7 select_reduce_fusion
  18.7 0.1 reshape.125
  18.8 0.1 broadcast_in_dim.38
  18.9 5.8 %gather_fusion = bf16[1280,1792]{1,0:T(8,128)(2,1)} fusion(bf16[128,1792]{1,0:T(8,128)(2,1)S(1)} %copy-done, s32[2048]{0:T(1024)S(1)} %pad_clamp_fusion), kind=kCustom, calls=%fused_computation | custom fusion | bytes 9180160 | tf_op jit(solution)/shard_map/gather | solution.py:280
  24.7 2.7 broadcast_select_fusion
  27.4 63.4 %all_to_all.5 = bf16[32,40,1792]{2,1,0:T(8,128)(2,1)} all-to-all(bf16[32,40,1792]{2,1,0:T(8,128)(2,1)S(1)} %broadcast_select_fusion), channel_id=1, replica_groups=mesh['aa'=8,'ba'=4,'col'=4] {'aa','col'}, dimensions={0} | all-to-all | bytes 9175040 | tf_op jit(solution)/shard_map/all_to_all | solution.py:282
  90.9 0.6 copy-done.1
  91.5 38.2 %all-gather = s32[4096,16]{0,1:T(8,128)S(1)} all-gather(s32[128,16]{0,1:T(8,128)S(1)} %pad_add_fusion.1), channel_id=2, replica_groups=mesh['aa'=8,'ba'=4,'col'=4] {'aa','col'}, dimensions={0}, use_global_device_ids=true | all-gather | bytes 270336 | tf_op jit(solution)/shard_map/all_gather | solution.py:273
  129.9 0.1 convolution_convert_fusion.1
  130.1 0.3 select_reduce_fusion.1
  130.5 0.1 convolution_convert_fusion
  130.8 0.3 copy.26
  131.1 0.5 and.76
  131.6 1.1 and.77
  132.7 1.0 copy.28
  133.7 0.1 and.78
  133.8 0.2 copy.27
  134.0 1.3 and_convert_fusion.spread_ref
  135.3 122.1 %all-gather.3.cloned.1.call-done = bf16[32,40,7168]{2,1,0:T(8,128)(2,1)} async-done(((bf16[32,40,1792]{2,1,0:T(8,128)(2,1)}), bf16[32,40,7168]{2,1,0:T(8,128)(2,1)}) %all-gather.3.cloned.1.call-update) | async-done | bytes 18350096 | tf_op jit(solution)/shard_map/all_gather | solution.py:281
  257.4 14.6 %fusion.2 = f32[1280,512]{1,0:T(8,128)S(1)} fusion(bf16[1280,7168]{1,0:T(8,128)(2,1)} %bitcast.80, bf16[1,7168,512]{2,1,0:T(8,128)(2,1)} %param.9), kind=kOutput, calls=%fused_computation.3 | convolution fusion | flops 9395240960 | bytes 28311552 | tf_op jit(solution)/shard_map/dot_general | solution.py:288
  272.0 15.9 %fusion.11 = bf16[1280,512]{1,0:T(8,128)(2,1)S(1)} fusion(bf16[1280,7168]{1,0:T(8,128)(2,1)} %bitcast.81, bf16[1,7168,512]{2,1,0:T(8,128)(2,1)} %param.10, f32[1280,512]{1,0:T(8,128)S(1)} %fusion.2, f32[1280]{0:T(1024)S(1)} %mul.53), kind=kOutput, calls=%fused_computation.11 | convolution fusion | flops 9399828480 | bytes 29627392 | tf_op jit(solution)/shard_map/dot_general | solution.py:289
  287.9 1.2 constant_dynamic-slice_fusion.2
  289.1 147.9 %combine.1 = bf16[128,1792]{1,0:T(8,128)(2,1)} custom-call(bf16[640,512]{1,0:T(8,128)(2,1)} %bitcast.68, bf16[640,512]{1,0:T(8,128)(2,1)} %bitcast.67, bf16[512,7168]{1,0:T(8,128)(2,1)} %bitcast.66, bf16[8,256,160]{2,1,0:T(8,128)(2,1)} %and_convert_fusion.spread_ref), custom_call_target="tpu_custom_call" | custom-call | tf_op jit(solution)/shard_map/combine/pallas_call | solution.py:222
  437.0 1.8 copy.38
  (31 shorter events, 0.7 us)
Async XLA Ops:
  6.5 12.3 %copy-start = (bf16[128,1792]{1,0:T(8,128)(2,1)S(1)}, bf16[128,1792]{1,0:T(8,128)(2,1)}, u32[]{:S(2)}) copy-start(bf16[128,1792]{1,0:T(8,128)(2,1)} %param.6) | copy-start | bytes 1376260
  6.5 250.9 %all-gather.3.cloned.1.call-start = ((), (), s32[]{:S(2)}) async-start(), calls=%async_computation.1 | async-start | bytes 22937600 | tf_op jit(solution)/shard_map/all_gather | solution.py:281
  90.8 0.7 copy-start.1
  90.8 0.7 copy-start.2
Sparse Core Ops, SparseCore 0:
  91.0 166.3 all-gather.2

commit v2 on v1

--- a/solution.py
+++ b/solution.py
@@ -14,19 +14,6 @@
 ORDERS = (("x", "y", "z"), ("y", "z", "x"), ("z", "x", "y"))
 
 
-def route_tables(routing, experts, slots_each, top):
-    flat = routing.reshape(-1)
-    onehot = (flat[:, None] == jnp.arange(experts, dtype=jnp.int32)[None, :]).astype(jnp.int32)
-    before = jnp.cumsum(onehot, axis=0) - onehot
-    pos = jnp.sum(before * onehot, axis=1)
-    slot = flat * slots_each + pos
-    matched = slot[:, None] == jnp.arange(experts * slots_each, dtype=jnp.int32)[None, :]
-    owner = jnp.arange(flat.shape[0], dtype=jnp.int32) // top
-    slot_token = jnp.sum(jnp.where(matched, owner[:, None], 0), axis=0)
-    live = jnp.any(matched, axis=0)
-    return (slot, slot_token.reshape(experts, slots_each), live.reshape(experts, slots_each))
-
-
 def place():
     aa = lax.axis_index("aa")
     z, core = aa // 2, aa % 2
@@ -49,7 +36,265 @@
     pl.semaphore_wait(barrier, 7)
 
 
-def combine_kernel(slots, own_ref, other_ref, down_ref, spread_ref, out_ref,
+def pick_tables(core_groups, experts, put_pick, put_gain):
+    lane = lax.broadcasted_iota(jnp.int32, (128, 128), 1)
+    row = lax.broadcasted_iota(jnp.int32, (128, 128), 0)
+    before = (row < lane).astype(bf16)
+    slot_row = lax.broadcasted_iota(jnp.int32, (80, 256), 0)
+    half_lane = lax.broadcasted_iota(jnp.int32, (80, 256), 1)
+    second_row, second_lane = slot_row >= 40, half_lane >= 128
+    position = jnp.where(second_row, slot_row - 40, slot_row).astype(f32)
+    same = second_row == second_lane
+    for source, expert in enumerate(experts):
+        taken, pos, gain = [], [], []
+        for block in core_groups:
+            block = block.astype(f32)
+            code = block[8:16] * 256.0 + block[16:24]
+            weight = route_scale * code / jnp.sum(code, axis=0, keepdims=True)
+            named = block[0:8] == expert
+            hit = jnp.max(jnp.where(named, 1.0, 0.0), axis=0, keepdims=True)
+            taken.append(hit)
+            wide = jnp.broadcast_to(hit, (8, 128)).astype(bf16)
+            pos.append(jnp.dot(wide, before, preferred_element_type=f32)[0:1])
+            gain.append(jnp.sum(jnp.where(named, weight, 0.0), axis=0, keepdims=True))
+        taken, pos, gain = (jnp.concatenate(v, axis=1) for v in (taken, pos, gain))
+        hot = same & (pos == position) & (taken > 0.5)
+        put_pick(source, jnp.where(hot, 1.0, 0.0).astype(bf16))
+        put_gain(source, jnp.broadcast_to(jnp.sum(jnp.where(hot, gain, 0.0), axis=1, keepdims=True), (80, 128)))
+
+
+def dispatch_kernel(slots, tok_ref, meta_ref, gate_hbm, up_hbm, own_ref, other_ref, pick_ref,
+                    gate_ref, up_ref, total, out1, out2, out3, rows_own, rows_send, rows_got, gain_own, gain_send, gain_got,
+                    send_sem, recv_sem, pair_send, pair_recv, gain_sem, load_sem, credit):
+    me, core = place()
+    partner = {"aa": me["z"] * 2 + (1 - core)}
+    outs = (out1, out2, out3)
+    quarter = tok_ref.shape[1]
+    loads = [pltpu.make_async_copy(gate_hbm, gate_ref, load_sem.at[0]), pltpu.make_async_copy(up_hbm, up_ref, load_sem.at[1])]
+    for load in loads:
+        load.start()
+    greet(me, core)
+
+    def tile_of(r, slot):
+        return pl.multiple_of((slot * 3 + (r + 1) % 3 - 1) * TILE, TILE)
+
+    def ring(r, phase, slot, kind):
+        p = lax.rem(slot, outs[phase].shape[1])
+        buf = outs[phase].at[r, p]
+        b = outs[phase].shape[2] // 4
+        h = b // 2
+        axis = ORDERS[r][phase]
+        src, dst, step = (
+            (pl.ds(0, b), pl.ds(3 * b, b), 1),
+            (pl.ds(0, b), pl.ds(b, b), -1),
+            (pl.ds(3 * b, h), pl.ds(2 * b, h), 1),
+            (pl.ds(b + h, h), pl.ds(2 * b + h, h), -1),
+        )[kind]
+        return pltpu.make_async_remote_copy(
+            src_ref=buf.at[src], dst_ref=buf.at[dst], send_sem=send_sem.at[r, phase, kind, p],
+            recv_sem=recv_sem.at[r, phase, kind, p], device_id=peer(me, core, axis, step), device_id_type=MESH)
+
+    def pair(r, slot):
+        p = lax.rem(slot, 2)
+        return pltpu.make_async_remote_copy(
+            src_ref=rows_send.at[r], dst_ref=rows_got.at[r, p], send_sem=pair_send.at[r], recv_sem=pair_recv.at[r, p],
+            device_id=partner, device_id_type=MESH)
+
+    gains = pltpu.make_async_remote_copy(
+        src_ref=gain_send, dst_ref=gain_got, send_sem=gain_sem.at[0], recv_sem=gain_sem.at[1],
+        device_id=partner, device_id_type=MESH)
+
+    def begin(r, phase, slot):
+        @pl.when(slot >= outs[phase].shape[1])
+        def _():
+            pl.semaphore_wait(credit.at[r, phase, 0], 1)
+            pl.semaphore_wait(credit.at[r, phase, 1], 1)
+
+        ring(r, phase, slot, 0).start()
+        ring(r, phase, slot, 1).start()
+
+    def open_tile(r, slot):
+        p = lax.rem(slot, 2)
+
+        def tokens():
+            out1[r, p, 0:128, :] = tok_ref[:, pl.ds(tile_of(r, slot), TILE)]
+
+        if r == 2:
+            @pl.when(slot == 0)
+            def _():
+                out1[r, p, 0:128, :] = meta_ref[...]
+
+            pl.when(slot > 0)(tokens)
+        else:
+            tokens()
+        begin(r, 0, slot)
+
+    def middle(r, phase, slot):
+        ring(r, phase, slot, 0).wait_recv()
+        ring(r, phase, slot, 2).start()
+        ring(r, phase, slot, 1).wait_recv()
+        ring(r, phase, slot, 3).start()
+
+    def close(r, phase, slot):
+        for kind in range(4):
+            ring(r, phase, slot, kind).wait_send()
+
+        @pl.when(slot + outs[phase].shape[1] < slots[r])
+        def _():
+            axis = ORDERS[r][phase]
+            pl.semaphore_signal(credit.at[r, phase, 0], inc=1, device_id=peer(me, core, axis, 1), device_id_type=MESH)
+            pl.semaphore_signal(credit.at[r, phase, 1], inc=1, device_id=peer(me, core, axis, -1), device_id_type=MESH)
+
+    def finish(r, phase, slot):
+        ring(r, phase, slot, 2).wait_recv()
+        ring(r, phase, slot, 3).wait_recv()
+        src, dst = outs[phase], outs[phase + 1]
+        p, q = lax.rem(slot, src.shape[1]), lax.rem(slot, dst.shape[1])
+
+        @pl.loop(0, src.shape[2] // 512)
+        def _(i):
+            at = pl.multiple_of(i * 512, 512)
+            dst[r, q, pl.ds(at, 512), :] = src[r, p, pl.ds(at, 512), :]
+        begin(r, phase + 1, slot)
+        close(r, phase, slot)
+
+    def block_of(r, z, x, y):
+        weight = {axis: 4 ** ORDERS[r].index(axis) for axis in "xyz"}
+        at = sum(lax.rem(there - me[axis] + 4, 4) * weight[axis] for axis, there in (("z", z), ("x", x), ("y", y)))
+        return pl.multiple_of(at * 128, 128)
+
+    def tables(r, slot):
+        experts = [(((me["z"] * 2 + c) * 4) + me["x"]).astype(f32) for c in (core, 1 - core)]
+
+        @pl.loop(0, 8)
+        def _(n):
+            z = n // 2
+            blocks = [out3[r, 0, pl.ds(block_of(r, z, lax.rem(n, 2) * 2 + half, me["y"]), 32), :] for half in range(2)]
+
+            def put_pick(source, hot):
+                pick_ref[n, source * 80:source * 80 + 80, :] = hot
+
+            def put_gain(source, gain):
+                (gain_own, gain_send)[source][n] = gain
+            pick_tables(blocks, experts, put_pick, put_gain)
+        gains.start()
+
+    def select(r, slot):
+        p = lax.rem(slot, out3.shape[1])
+
+        @pl.when(slot >= (2 if r == 2 else 1))
+        def _():
+            pair(r, slot - 1).wait_send()
+
+        @pl.loop(0, 8)
+        def _(n):
+            z = n // 2
+            wide = [jnp.concatenate([out3[r, p, pl.ds(block_of(r, z, lax.rem(n, 2) * 2 + half, q), 128), :] for q in range(4)], axis=1)
+                    for half in range(2)]
+            rows = jnp.dot(pick_ref[n], jnp.concatenate(wide, axis=0), preferred_element_type=f32).astype(bf16)
+            at = pl.ds(pl.multiple_of(n * 80, 16), 80)
+            rows_own[r, at, :] = rows[0:80]
+            rows_send[r, at, :] = rows[80:160]
+        pair(r, slot).start()
+
+        @pl.when(slot == slots[r] - 1)
+        def _():
+            pair(r, slot).wait_send()
+
+    def gather(r, slot):
+        ring(r, 2, slot, 2).wait_recv()
+        ring(r, 2, slot, 3).wait_recv()
+        if r == 2:
+            pl.when(slot == 0)(lambda: tables(r, slot))
+            pl.when(slot > 0)(lambda: select(r, slot))
+        else:
+            select(r, slot)
+        close(r, 2, slot)
+
+    def multiply(r, slot):
+        p = lax.rem(slot, 2)
+
+        def work():
+            pair(r, slot).wait_recv()
+            first = tile_of(r, slot)
+            for w_ref, col in ((gate_ref, 0), (up_ref, 512)):
+                w = jnp.concatenate([w_ref[pl.ds(pl.multiple_of(q * quarter + first, TILE), TILE), :] for q in range(4)], axis=0)
+                total[0, :, col:col + 512] += jnp.dot(rows_own[r], w, preferred_element_type=f32)
+                total[1, :, col:col + 512] += jnp.dot(rows_got[r, p], w, preferred_element_type=f32)
+
+        if r == 2:
+            pl.when(slot > 0)(work)
+        else:
+            work()
+
+    def stage(step, delay, body):
+        for r in (2, 0, 1):
+            slot = step - delay
+
+            @pl.when((slot >= 0) & (slot < slots[r]))
+            def _():
+                body(r, slot)
+
+    @pl.loop(0, max(slots) + 6)
+    def _(step):
+        stage(step, 5, lambda r, s: middle(r, 2, s))
+        stage(step, 4, lambda r, s: finish(r, 1, s))
+        stage(step, 3, lambda r, s: middle(r, 1, s))
+        stage(step, 2, lambda r, s: finish(r, 0, s))
+        stage(step, 1, lambda r, s: middle(r, 0, s))
+        stage(step, 0, open_tile)
+        stage(step, 6, gather)
+
+        @pl.when(step == 6)
+        def _():
+            total[...] = jnp.zeros_like(total)
+            for load in loads:
+                load.wait()
+
+        stage(step, 6, multiply)
+
+    gains.wait()
+
+    @pl.loop(0, 8)
+    def _(n):
+        at = pl.ds(pl.multiple_of(n * 80, 16), 80)
+        for half, ref, gain in ((0, own_ref, gain_own), (1, other_ref, gain_got)):
+            gate = total[half, at, 0:512]
+            upper = total[half, at, 512:1024]
+            ref[at, :] = (jax.nn.silu(gate) * upper * gain[n][:, 0:1]).astype(bf16)
+
+
+def dispatch(tokens, meta, gate, up):
+    quarter = tokens.shape[1]
+    count = quarter // TILE + 1
+    slots = tuple((count - (r + 1) % 3 + 2) // 3 for r in range(3))
+    vmem = pl.BlockSpec(memory_space=pltpu.VMEM)
+    hbm = pl.BlockSpec(memory_space=pl.ANY)
+    hidden = jax.ShapeDtypeStruct((640, 512), bf16)
+    return pl.pallas_call(
+        functools.partial(dispatch_kernel, slots),
+        out_shape=(hidden, hidden, jax.ShapeDtypeStruct((8, 160, 256), bf16)),
+        in_specs=[vmem, vmem, hbm, hbm],
+        out_specs=(vmem,) * 3,
+        scratch_shapes=[
+            pltpu.VMEM(gate.shape, bf16), pltpu.VMEM(up.shape, bf16), pltpu.VMEM((2, 640, 1024), f32),
+            pltpu.VMEM((3, 2, 512, TILE), bf16), pltpu.VMEM((3, 2, 2048, TILE), bf16), pltpu.VMEM((3, 3, 8192, TILE), bf16),
+            pltpu.VMEM((3, 640, 4 * TILE), bf16), pltpu.VMEM((3, 640, 4 * TILE), bf16), pltpu.VMEM((3, 2, 640, 4 * TILE), bf16),
+            pltpu.VMEM((8, 80, 128), f32), pltpu.VMEM((8, 80, 128), f32), pltpu.VMEM((8, 80, 128), f32),
+            pltpu.SemaphoreType.DMA((3, 3, 4, 3)),
+            pltpu.SemaphoreType.DMA((3, 3, 4, 3)),
+            pltpu.SemaphoreType.DMA((3,)),
+            pltpu.SemaphoreType.DMA((3, 2)),
+            pltpu.SemaphoreType.DMA((2,)),
+            pltpu.SemaphoreType.DMA((2,)),
+            pltpu.SemaphoreType.REGULAR((3, 3, 2)),
+        ],
+        compiler_params=pltpu.CompilerParams(collective_id=0, has_side_effects=True, vmem_limit_bytes=66000000),
+        name="dispatch",
+    )(tokens, meta, gate, up)
+
+
+def combine_kernel(slots, own_ref, other_ref, down_ref, pick_ref, out_ref,
                    send_rows, pair_rows, in1, in2, in3, got1, got2, got3, more1, more2, more3,
                    send_sem, recv_sem, pair_send, pair_recv, credit):
     me, core = place()
@@ -124,7 +369,7 @@
         @pl.loop(0, 8)
         def _(n):
             z = n // 2
-            rows = jnp.dot(spread_ref[n], pair_rows[r, p, n], preferred_element_type=f32).astype(bf16)
+            rows = lax.dot_general(pick_ref[n], pair_rows[r, p, n], (((0,), (0,)), ((), ())), preferred_element_type=f32).astype(bf16)
             to_z = lax.rem(z - me["z"] + 4, 4) * weight["z"]
             for half in range(2):
                 x = lax.rem(n, 2) * 2 + half
@@ -210,7 +455,7 @@
         stage(step, 0, project)
 
 
-def combine(own, other, down, spread):
+def combine(own, other, down, pick):
     quarter = down.shape[1] // 4
     count = quarter // TILE
     slots = tuple((count - r + 2) // 3 for r in range(3))
@@ -238,60 +483,14 @@
         ],
         compiler_params=pltpu.CompilerParams(collective_id=1, has_side_effects=True, vmem_limit_bytes=66000000),
         name="combine",
-    )(own, other, down, spread)
-
-
-def expert_tables(routing, weight, expert, cap):
-    named = routing == expert
-    taken = jnp.any(named, axis=2)
-    ones = taken.astype(f32)
-    rank = jnp.arange(128)
-    pos = jnp.dot(ones, (rank[:, None] < rank[None, :]).astype(f32)).astype(jnp.int32)
-    hot = taken[:, :, None] & (pos[:, :, None] == jnp.arange(cap, dtype=jnp.int32)[None, None, :])
-    gain = jnp.sum(jnp.where(named, weight, 0.0), axis=2)
-    return hot, jnp.sum(jnp.where(hot, gain[:, :, None], 0.0), axis=1)
-
-
-def spread_matrix(hot_own, hot_other, core):
-    def mine(hot):
-        by = hot.reshape(4, 2, 2, 2, 128, 40)
-        return lax.dynamic_index_in_dim(by, core, 1, keepdims=False)
-    both = jnp.stack([mine(hot_own), mine(hot_other)], axis=4)
-    eye = jnp.eye(2, dtype=bool)
-    wide = both[:, :, :, :, :, None, :] & eye[None, None, :, None, None, :, None]
-    return wide.reshape(8, 256, 160).astype(bf16)
+    )(own, other, down, pick)
 
 
 def on_device(tokens, routing, gate_codes, w_gate, w_up, w_down):
-    experts = lax.axis_size("aa") * lax.axis_size("col")
-    tok_rows = tokens.shape[0]
-    top = routing.shape[1]
-    cap = min(tok_rows, 5 * tok_rows * top // (4 * experts))
-    aa, col = lax.axis_index("aa"), lax.axis_index("col")
-    core = aa % 2
-    slot, slot_token, live = route_tables(routing, experts, cap, top)
-    all_codes = lax.all_gather(jnp.concatenate([routing, gate_codes], axis=1), ("aa", "col"), axis=0, tiled=False)
-    all_routing = all_codes[:, :, :top]
-    codes = all_codes[:, :, top:].astype(f32)
-    weight = route_scale * codes / jnp.sum(codes, axis=2, keepdims=True)
-    hot_own, gain_own = expert_tables(all_routing, weight, aa * 4 + col, cap)
-    hot_other, _ = expert_tables(all_routing, weight, (aa + 1 - 2 * core) * 4 + col, cap)
-    spread = spread_matrix(hot_own, hot_other, core)
-    outgoing = jnp.where(live[:, :, None], tokens[slot_token], jnp.zeros((), bf16))
-    full_rows = lax.all_gather(
-        lax.all_to_all(outgoing, ("aa", "col"), split_axis=0, concat_axis=0, tiled=True),
-        "ba",
-        axis=2,
-        tiled=True,
-    )
-    rows = full_rows.reshape(experts * cap, full_rows.shape[2])
-    gate = jnp.dot(rows, w_gate[0], preferred_element_type=f32)
-    upper = jnp.dot(rows, w_up[0], preferred_element_type=f32)
-    hidden = (jax.nn.silu(gate) * upper * gain_own.reshape(-1, 1)).astype(bf16)
-    by_core = hidden.reshape(4, 2, 160, hidden.shape[1])
-    own = lax.dynamic_index_in_dim(by_core, core, 1, keepdims=False).reshape(640, -1)
-    other = lax.dynamic_index_in_dim(by_core, 1 - core, 1, keepdims=False).reshape(640, -1)
-    return combine(own, other, w_down[0], spread)
+    codes = jnp.concatenate([routing, gate_codes // 256, gate_codes % 256], axis=1).astype(bf16).T
+    meta = jnp.pad(codes, ((0, 128 - codes.shape[0]), (0, 0)))
+    own, other, pick = dispatch(tokens, meta, w_gate[0], w_up[0])
+    return combine(own, other, w_down[0], pick)
 
 
 def solution(mesh):

time: 446 us -> 303 us (0.68)
  Pallas kernels: 148 us -> 299 us
  waiting for transfers between devices: 122 us -> 0 us
  blocking collectives: 102 us -> 0 us
  matrix products: 30.8 us -> 0 us
  other arithmetic: 15.1 us -> 1.39 us
  between operations: 13.7 us -> 0.02 us
  local copies, waits for them, and re-layouts: 14.4 us -> 2.44 us
    pallas_call x0 -> x1, Pallas kernels: none -> 150 us  [dispatch(): pl.pallas_call(functools.partial(dispatch_kernel, slots), out_shape=(hidd...]
    all_gather x1 -> x0, waiting for transfers between devices: 122 us -> none  [on_device(): lax.all_gather(lax.all_to_all(outgoing, ('aa', 'col'), split_axis=0, conc...]
    all_to_all x1 -> x0, blocking collectives: 63.4 us -> none  [on_device(): lax.all_to_all(outgoing, ('aa', 'col'), split_axis=0, concat_axis=0, tile...]
    all_gather x1 -> x0, blocking collectives: 38.2 us -> none  [on_device(): lax.all_gather(jnp.concatenate([routing, gate_codes], axis=1), ('aa', 'co...]
    dot_general x4 -> x0, matrix products: 30.8 us -> none  [the longest x1 15.9 us: on_device(): upper = jnp.dot(rows, w_up[0], preferred_element_type=f32)]
    another operation x6 -> x2, other arithmetic: 9.3 us -> 1.39 us
    gather x1 -> x0, local copies, waits for them, and re-layouts: 5.8 us -> none  [on_device(): tokens[slot_token]]
  transfers between devices with their start and end apart: 1 -> 0, of which waited for: 1 -> 0; matrix products, arithmetic and copies ran while one was open for 1% -> 0% of each run, Pallas kernels for 0% -> 0%
where the time goes in v2:
time: 303 us; the launch traced here: 302 us
  Pallas kernels  299 us (99%)
    pallas_call x1, Pallas kernels, dispatch(): pl.pallas_call(functools.partial(dispatch_kernel, slots), out_shape=(hidd...  150 us
    pallas_call x1, Pallas kernels, combine(): pl.pallas_call(functools.partial(combine_kernel, slots), out_shape=jax.Sh...  149 us

profile of v2, /device:TPU:0, one launch (start us, length us, event | category | flops | bytes accessed | tf_op | source)
XLA Modules:
  0.0 302.5 jit_solution(8055992806616383320)
XLA Ops:
  0.0 0.7 convert.9
  0.7 0.7 fusion
  1.4 0.6 pad.4.meta_ref
  2.0 149.5 %dispatch.1 = (bf16[640,512]{1,0:T(8,128)(2,1)}, bf16[640,512]{1,0:T(8,128)(2,1)}, bf16[8,160,256]{2,1,0:T(8,128)(2,1)}) custom-call(bf16[128,1792]{1,0:T(8,128)(2,1)} %tok_ref.1, bf16[128,128]{1,0:T(8,128)(2,1)} %pad.4.meta_ref, bf16[7168,512]{1,0:T(8,128)(2,1)} %bitcast.6, bf16[7168,512]{1,0:T(8,128)(2,1)} %bitcast.7), custom_call_target="tpu_custom_call" | custom-call | tf_op jit(solution)/shard_map/dispatch/pallas_call | solution.py:274
  151.6 149.1 %combine.1 = bf16[128,1792]{1,0:T(8,128)(2,1)} custom-call(bf16[640,512]{1,0:T(8,128)(2,1)} %get-tuple-element.8.own_ref, bf16[640,512]{1,0:T(8,128)(2,1)} %get-tuple-element.9.other_ref, bf16[512,7168]{1,0:T(8,128)(2,1)} %bitcast.5, bf16[8,160,256]{2,1,0:T(8,128)(2,1)} %get-tuple-element.10.pick_ref), custom_call_target="tpu_custom_call" | custom-call | tf_op jit(solution)/shard_map/combine/pallas_call | solution.py:467
  300.6 1.8 copy.8
  (1 shorter events, 0.0 us)

commit v3 on v0

v3 whole, which is shorter than its diff:
```python
import functools
import jax
import jax.numpy as jnp
from jax import lax
from jax.experimental import pallas as pl
from jax.experimental.pallas import tpu as pltpu
from jax.sharding import PartitionSpec as P

MESH = pl.DeviceIdType.MESH
route_scale = 2.827
bf16 = jnp.bfloat16
f32 = jnp.float32
TILE = 128
STREAMS = ((("z", "x", "y"), 0, 4), (("x", "z", "y"), 4, 4), (("y", "z", "x"), 8, 3), (("y", "x", "z"), 11, 3))
PACKED = 2
RIGHT, LEFT = 1, -1


def place():
    aa = lax.axis_index("aa")
    return {"z": aa // 2, "y": lax.axis_index("ba"), "x": lax.axis_index("col")}, aa % 2


def peer(me, core, axis, step):
    at = lax.rem(me[axis] + (step + 4), 4)
    if axis == "z":
        return {"aa": at * 2 + core}
    return {"ba": at} if axis == "y" else {"col": at}


def greet(me, core):
    barrier = pltpu.get_barrier_semaphore()
    for axis in "xyz":
        for step in (RIGHT, LEFT):
            pl.semaphore_signal(barrier, inc=1, device_id=peer(me, core, axis, step), device_id_type=MESH)
    pl.semaphore_signal(barrier, inc=1, device_id={"aa": me["z"] * 2 + (1 - core)}, device_id_type=MESH)
    pl.semaphore_wait(barrier, 7)


def grant(me, core, credit, phase, axis):
    pl.semaphore_signal(credit.at[phase, 0], inc=1, device_id=peer(me, core, axis, RIGHT), device_id_type=MESH)
    pl.semaphore_signal(credit.at[phase, 1], inc=1, device_id=peer(me, core, axis, LEFT), device_id_type=MESH)


def spend(credit, phase):
    pl.semaphore_wait(credit.at[phase, 0], 1)
    pl.semaphore_wait(credit.at[phase, 1], 1)


def tiles(rows, body):
    size = min(rows, 128 if rows % 256 else 256)
    if rows == size:
        body(0, size)
    else:
        @pl.loop(0, rows // size)
        def _(i):
            body(pl.multiple_of(i * size, size), size)


def block_at(me, weights, there):
    at = sum(lax.rem(spot - me[axis] + 4, 4) * weights[axis] for axis, spot in there.items())
    return pl.multiple_of(at * 128, 128)


def pick_tables(blocks, experts, put_pick, put_gain):
    lane = lax.broadcasted_iota(jnp.int32, (128, 128), 1)
    row = lax.broadcasted_iota(jnp.int32, (128, 128), 0)
    before = (row < lane).astype(bf16)
    slot_row = lax.broadcasted_iota(jnp.int32, (80, 256), 0)
    half_lane = lax.broadcasted_iota(jnp.int32, (80, 256), 1)
    second_row, second_lane = slot_row >= 40, half_lane >= 128
    position = jnp.where(second_row, slot_row - 40, slot_row).astype(f32)
    same = second_row == second_lane
    for source, expert in enumerate(experts):
        taken, pos, gain = [], [], []
        for block in blocks:
            block = block.astype(f32)
            code = block[8:16] * 256.0 + block[16:24]
            weight = route_scale * code / jnp.sum(code, axis=0, keepdims=True)
            named = block[0:8] == expert
            hit = jnp.max(jnp.where(named, 1.0, 0.0), axis=0, keepdims=True)
            taken.append(hit)
            wide = jnp.broadcast_to(hit, (8, 128)).astype(bf16)
            pos.append(jnp.dot(wide, before, preferred_element_type=f32)[0:1])
            gain.append(jnp.sum(jnp.where(named, weight, 0.0), axis=0, keepdims=True))
        taken, pos, gain = (jnp.concatenate(v, axis=1) for v in (taken, pos, gain))
        hot = same & (pos == position) & (taken > 0.5)
        put_pick(source, jnp.where(hot, 1.0, 0.0).astype(bf16))
        put_gain(source, jnp.broadcast_to(jnp.sum(jnp.where(hot, gain, 0.0), axis=1, keepdims=True), (80, 128)))


class Gather:
    def __init__(self, me, core, axes, outs, sends, recvs, credit, slots):
        self.me, self.core, self.axes, self.outs = me, core, axes, outs
        self.sends, self.recvs, self.credit, self.slots = sends, recvs, credit, slots

    def depth(self, phase):
        return self.outs[phase].shape[0]

    def copy(self, phase, slot, kind):
        p = lax.rem(slot, self.depth(phase))
        buf = self.outs[phase].at[p]
        b = self.outs[phase].shape[1] // 4
        h = b // 2
        src, dst, step = (
            (pl.ds(0, b), pl.ds(3 * b, b), RIGHT),
            (pl.ds(0, b), pl.ds(b, b), LEFT),
            (pl.ds(3 * b, h), pl.ds(2 * b, h), RIGHT),
            (pl.ds(b + h, h), pl.ds(2 * b + h, h), LEFT),
        )[kind]
        return pltpu.make_async_remote_copy(
            src_ref=buf.at[src], dst_ref=buf.at[dst], send_sem=self.sends[phase].at[kind, p], recv_sem=self.recvs[phase].at[kind, p],
            device_id=peer(self.me, self.core, self.axes[phase], step), device_id_type=MESH)

    def begin(self, phase, slot):
        if self.slots > self.depth(phase):
            pl.when(slot >= self.depth(phase))(lambda: spend(self.credit, phase))
        self.copy(phase, slot, 0).start()
        self.copy(phase, slot, 1).start()

    def middle(self, phase, slot):
        self.copy(phase, slot, 0).wait_recv()
        self.copy(phase, slot, 2).start()
        self.copy(phase, slot, 1).wait_recv()
        self.copy(phase, slot, 3).start()

    def arrive(self, phase, slot):
        self.copy(phase, slot, 2).wait_recv()
        self.copy(phase, slot, 3).wait_recv()

    def close(self, phase, slot):
        for kind in range(4):
            self.copy(phase, slot, kind).wait_send()
        if self.slots > self.depth(phase):
            pl.when(slot + self.depth(phase) < self.slots)(
                lambda: grant(self.me, self.core, self.credit, phase, self.axes[phase]))

    def forward(self, phase, slot):
        src, dst = self.outs[phase], self.outs[phase + 1]
        p, q = lax.rem(slot, src.shape[0]), lax.rem(slot, dst.shape[0])

        def move(at, n):
            dst[q, pl.ds(at, n), :] = src[p, pl.ds(at, n), :]
        tiles(src.shape[1], move)


def dispatch_kernel(tok_ref, meta_ref, gate_hbm, up_hbm, own_ref, other_ref, pick_ref,
                    gate_ref, up_ref, total, gain_own, gain_send, gain_got, gain_sem, load_sem, credit, *rest):
    rest = list(rest)

    def take(n):
        taken = rest[:n]
        del rest[:n]
        return taken

    me, core = place()
    partner = {"aa": me["z"] * 2 + (1 - core)}
    quarter = tok_ref.shape[1]
    loads = [pltpu.make_async_copy(gate_hbm, gate_ref, load_sem.at[0]), pltpu.make_async_copy(up_hbm, up_ref, load_sem.at[1])]
    for load in loads:
        load.start()
    greet(me, core)
    rings, wares = [], []
    for s, (axes, _, slots) in enumerate(STREAMS):
        rings.append(Gather(me, core, axes, take(3), take(3), take(3), credit.at[s], slots))
        wares.append(take(3 if s < PACKED else 5))
    notes = Gather(me, core, ("x", "z"), take(2), take(2), take(2), None, 1)
    gains = pltpu.make_async_remote_copy(
        src_ref=gain_send, dst_ref=gain_got, send_sem=gain_sem.at[0], recv_sem=gain_sem.at[1],
        device_id=partner, device_id_type=MESH)

    def pair(s, slot, part=0):
        if s < PACKED:
            got, send, recv = wares[s]
            b = got.shape[2]
            src = rings[s].outs[2].at[lax.rem(slot, rings[s].depth(2)), pl.ds(2 * b * part + b, b)]
            dst = got.at[lax.rem(slot, 2), part]
            send_at, recv_at = send.at[part], recv.at[lax.rem(slot, 2), part]
        else:
            _, src, got, send, recv = wares[s]
            dst = got.at[lax.rem(slot, 2)]
            send_at, recv_at = send.at[0], recv.at[lax.rem(slot, 2)]
        return pltpu.make_async_remote_copy(
            src_ref=src, dst_ref=dst, send_sem=send_at, recv_sem=recv_at, device_id=partner, device_id_type=MESH)

    def tile_of(s, slot):
        return pl.multiple_of((slot + STREAMS[s][1]) * TILE, TILE)

    def open_tile(s, slot):
        rings[s].outs[0][lax.rem(slot, 2), 0:128, :] = tok_ref[:, pl.ds(tile_of(s, slot), TILE)]
        rings[s].begin(0, slot)

    def pick(n, blocks):
        return jnp.dot(pick_ref[n], jnp.concatenate(blocks, axis=0), preferred_element_type=f32).astype(bf16)

    def pass_on(s, phase, slot):
        ring = rings[s]
        ring.arrive(phase, slot)
        if phase == 1 and s < PACKED:
            src, dst = ring.outs[1], ring.outs[2]
            p, q = lax.rem(slot, 2), lax.rem(slot, ring.depth(2))
            weights = {ring.axes[0]: 1, ring.axes[1]: 4}

            @pl.loop(0, 8)
            def _(n):
                blocks = [src[p, pl.ds(block_at(me, weights, {"z": n // 2, "x": lax.rem(n, 2) * 2 + half}), 128), :] for half in range(2)]
                rows = pick(n, blocks)
                at = pl.multiple_of(n * 80, 16)
                dst[q, pl.ds(at, 80), :] = rows[0:80]
                dst[q, pl.ds(at + 640, 80), :] = rows[80:160]
        else:
            ring.forward(phase, slot)
        ring.begin(phase + 1, slot)
        ring.close(phase, slot)

    def tables():
        experts = [(((me["z"] * 2 + c) * 4) + me["x"]).astype(f32) for c in (core, 1 - core)]

        @pl.loop(0, 8)
        def _(n):
            spots = [block_at(me, {"x": 1, "z": 4}, {"z": n // 2, "x": lax.rem(n, 2) * 2 + half}) // 4 for half in range(2)]
            blocks = [notes.outs[1][0, pl.ds(pl.multiple_of(at, 32), 32), :] for at in spots]

            def put_pick(source, hot):
                pick_ref[n, source * 80:source * 80 + 80, :] = hot

            def put_gain(source, gain):
                (gain_own, gain_send)[source][n] = gain
            pick_tables(blocks, experts, put_pick, put_gain)
        gains.start()

    def collect(s, slot):
        ring = rings[s]
        ring.arrive(2, slot)
        if s < PACKED:
            for part in range(4):
                pair(s, slot, part).start()
            return
        own, send = wares[s][:2]
        p = lax.rem(slot, ring.depth(2))
        weights = {axis: 4 ** i for i, axis in enumerate(ring.axes)}
        pl.when(slot >= 1)(lambda: pair(s, slot - 1).wait_send())

        @pl.loop(0, 8)
        def _(n):
            blocks = [jnp.concatenate([ring.outs[2][p, pl.ds(block_at(me, weights, {"z": n // 2, "x": lax.rem(n, 2) * 2 + half, "y": q}), 128), :]
                                       for q in range(4)], axis=1) for half in range(2)]
            rows = pick(n, blocks)
            at = pl.ds(pl.multiple_of(n * 80, 16), 80)
            own[at, :] = rows[0:80]
            send[at, :] = rows[80:160]
        pair(s, slot).start()
        pl.when(slot == ring.slots - 1)(lambda: pair(s, slot).wait_send())
        ring.close(2, slot)

    def multiply(s, slot):
        ring = rings[s]
        first = tile_of(s, slot)
        if s < PACKED:
            for part in range(4):
                pair(s, slot, part).wait_recv()
            got = wares[s][0]
            quarters = [lax.rem(me["y"] + part, 4) for part in range(4)]
            p = lax.rem(slot, ring.depth(2))
            rows = (jnp.concatenate([ring.outs[2][p, pl.ds(1280 * part, 640), :] for part in range(4)], axis=1),
                    jnp.concatenate([got[lax.rem(slot, 2), part] for part in range(4)], axis=1))
        else:
            pair(s, slot).wait_recv()
            quarters = range(4)
            rows = (wares[s][0][...], wares[s][2][lax.rem(slot, 2)])
        for w_ref, col in ((gate_ref, 0), (up_ref, 512)):
            w = jnp.concatenate([w_ref[pl.ds(pl.multiple_of(q * quarter + first, TILE), TILE), :] for q in quarters], axis=0)
            for half in range(2):
                total[half, :, col:col + 512] += jnp.dot(rows[half], w, preferred_element_type=f32)
        if s < PACKED:
            for part in range(4):
                pair(s, slot, part).wait_send()
            ring.close(2, slot)

    def stage(step, delay, body):
        for s, (_, _, slots) in enumerate(STREAMS):
            slot = step - delay
            pl.when((slot >= 0) & (slot < slots))(functools.partial(body, s, slot))

    def note(step, at, body):
        pl.when(step == at)(body)

    def note_open():
        notes.outs[0][0, 0:32, :] = meta_ref[...]
        notes.begin(0, 0)

    def note_pass():
        notes.arrive(0, 0)
        notes.forward(0, 0)
        notes.begin(1, 0)
        notes.close(0, 0)

    def note_end():
        notes.arrive(1, 0)
        tables()
        notes.close(1, 0)

    @pl.loop(0, max(slots for _, _, slots in STREAMS) + 6)
    def _(step):
        note(step, 4, note_end)
        note(step, 3, lambda: notes.middle(1, 0))
        note(step, 2, note_pass)
        note(step, 1, lambda: notes.middle(0, 0))
        note(step, 0, note_open)
        stage(step, 5, lambda s, slot: rings[s].middle(2, slot))
        stage(step, 4, lambda s, slot: pass_on(s, 1, slot))
        stage(step, 3, lambda s, slot: rings[s].middle(1, slot))
        stage(step, 2, lambda s, slot: pass_on(s, 0, slot))
        stage(step, 1, lambda s, slot: rings[s].middle(0, slot))
        stage(step, 0, open_tile)
        stage(step, 6, collect)

        @pl.when(step == 5)
        def _():
            total[...] = jnp.zeros_like(total)
            for load in loads:
                load.wait()

        stage(step, 6, multiply)

    gains.wait()

    @pl.loop(0, 8)
    def _(n):
        at = pl.ds(pl.multiple_of(n * 80, 16), 80)
        for half, ref, gain in ((0, own_ref, gain_own), (1, other_ref, gain_got)):
            gate = total[half, at, 0:512]
            upper = total[half, at, 512:1024]
            ref[at, :] = (jax.nn.silu(gate) * upper * gain[n][:, 0:1]).astype(bf16)


def rows_buffer(*shape):
    return pltpu.VMEM(shape + (TILE,), bf16)


def dispatch(tokens, meta, gate, up):
    vmem = pl.BlockSpec(memory_space=pltpu.VMEM)
    hbm = pl.BlockSpec(memory_space=pl.ANY)
    dma = pltpu.SemaphoreType.DMA
    hidden = jax.ShapeDtypeStruct((640, 512), bf16)
    scratch = [
        pltpu.VMEM(gate.shape, bf16), pltpu.VMEM(up.shape, bf16), pltpu.VMEM((2, 640, 1024), f32),
        pltpu.VMEM((8, 80, 128), f32), pltpu.VMEM((8, 80, 128), f32), pltpu.VMEM((8, 80, 128), f32),
        dma((2,)), dma((2,)), pltpu.SemaphoreType.REGULAR((len(STREAMS), 3, 2)),
    ]
    for s in range(len(STREAMS)):
        scratch += [rows_buffer(2, 512), rows_buffer(2, 2048), rows_buffer(3, 5120 if s < PACKED else 8192)]
        scratch += [dma((4, 2)), dma((4, 2)), dma((4, 3))] * 2
        if s < PACKED:
            scratch += [rows_buffer(2, 4, 640), dma((4,)), dma((2, 4))]
        else:
            scratch += [pltpu.VMEM((640, 512), bf16), pltpu.VMEM((640, 512), bf16), pltpu.VMEM((2, 640, 512), bf16), dma((1,)), dma((2,))]
    scratch += [rows_buffer(1, 128), rows_buffer(1, 512)] + [dma((4, 1))] * 4
    return pl.pallas_call(
        dispatch_kernel,
        out_shape=(hidden, hidden, jax.ShapeDtypeStruct((8, 160, 256), bf16)),
        in_specs=[vmem, vmem, hbm, hbm],
        out_specs=(vmem,) * 3,
        scratch_shapes=scratch,
        compiler_params=pltpu.CompilerParams(collective_id=0, has_side_effects=True, vmem_limit_bytes=66900000),
        name="dispatch",
    )(tokens, meta, gate, up)


class Reduce:
    def __init__(self, me, core, axes, ins, gots, mores, sends, recvs, credit, slots):
        self.me, self.core, self.axes = me, core, axes
        self.ins, self.gots, self.mores = ins, gots, mores
        self.sends, self.recvs, self.credit, self.slots = sends, recvs, credit, slots

    def copy(self, phase, slot, kind):
        p = lax.rem(slot, 2)
        buf = self.ins[phase].at[p]
        b = self.ins[phase].shape[1] // 4
        h = b // 2
        got, more = self.gots[phase], self.mores[phase]
        src, dst, step = (
            (pl.ds(b + h, b), got.at[p, 0], RIGHT),
            (pl.ds(2 * b + h, b), got.at[p, 1], LEFT),
            (pl.ds(b, h), more.at[p, 0], RIGHT),
            (pl.ds(3 * b + h, h), more.at[p, 1], LEFT),
        )[kind]
        return pltpu.make_async_remote_copy(
            src_ref=buf.at[src], dst_ref=dst, send_sem=self.sends.at[phase, kind, p], recv_sem=self.recvs.at[phase, kind, p],
            device_id=peer(self.me, self.core, self.axes[phase], step), device_id_type=MESH)

    def begin(self, phase, slot):
        pl.when(slot >= 2)(lambda: spend(self.credit, phase))
        self.copy(phase, slot, 0).start()
        self.copy(phase, slot, 1).start()

    def middle(self, phase, slot):
        p = lax.rem(slot, 2)
        buf, got = self.ins[phase], self.gots[phase]
        b = buf.shape[1] // 4
        h = b // 2
        for kind, base, skip in ((0, b, h), (1, 3 * b + h, 0)):
            self.copy(phase, slot, kind).wait_recv()

            def add(i, n):
                at = pl.ds(base + i, n)
                buf[p, at, :] = (buf[p, at, :].astype(f32) + got[p, kind, pl.ds(skip + i, n), :].astype(f32)).astype(bf16)
            tiles(h, add)
            self.copy(phase, slot, kind + 2).start()

    def finish(self, phase, slot, put):
        p = lax.rem(slot, 2)
        buf, got, more = self.ins[phase], self.gots[phase], self.mores[phase]
        b = buf.shape[1] // 4
        h = b // 2
        for kind, base, skip in ((0, 0, h), (1, h, 0)):
            self.copy(phase, slot, kind + 2).wait_recv()

            def add(i, n):
                at = base + i
                value = (buf[p, pl.ds(at, n), :].astype(f32) + got[p, 1 - kind, pl.ds(skip + i, n), :].astype(f32)
                         + more[p, kind, pl.ds(i, n), :].astype(f32))
                put(at, n, value.astype(bf16))
            tiles(h, add)

    def close(self, phase, slot):
        for kind in range(4):
            self.copy(phase, slot, kind).wait_send()
        pl.when(slot + 2 < self.slots)(lambda: grant(self.me, self.core, self.credit, phase, self.axes[phase]))


def combine_kernel(own_ref, other_ref, down_ref, pick_ref, out_ref, credit, *rest):
    rest = list(rest)

    def take(n):
        taken = rest[:n]
        del rest[:n]
        return taken

    me, core = place()
    partner = {"aa": me["z"] * 2 + (1 - core)}
    quarter = out_ref.shape[1]
    greet(me, core)
    rings, wares = [], []
    for s, (axes, _, slots) in enumerate(STREAMS):
        rings.append(Reduce(me, core, axes[::-1], take(3), take(3), take(3), *take(2), credit.at[s], slots))
        wares.append(take(6 if s < PACKED else 4))

    def pair(s, slot):
        p = lax.rem(slot, 2)
        if s < PACKED:
            _, src, got, _, send, recv = wares[s]
            dst = got.at[p]
        else:
            src, got, send, recv = wares[s]
            dst = got.at[p, :, pl.ds(80, 80)]
        return pltpu.make_async_remote_copy(
            src_ref=src, dst_ref=dst, send_sem=send.at[0], recv_sem=recv.at[p], device_id=partner, device_id_type=MESH)

    def tile_of(s, slot):
        return pl.multiple_of((slot + STREAMS[s][1]) * TILE, TILE)

    def project(s, slot):
        first = tile_of(s, slot)
        quarters = [lax.rem(me["y"] + part, 4) for part in range(4)] if s < PACKED else range(4)
        w = jnp.concatenate([down_ref[:, pl.ds(pl.multiple_of(q * quarter + first, TILE), TILE)] for q in quarters], axis=1)
        mine = jnp.dot(own_ref[...], w, preferred_element_type=f32).astype(bf16)
        if s < PACKED:
            for part in range(4):
                wares[s][0][part] = mine[:, part * TILE:(part + 1) * TILE]
        else:
            wares[s][1][lax.rem(slot, 2), :, 0:80, :] = mine.reshape(8, 80, 4 * TILE)
        pl.when(slot >= 1)(lambda: pair(s, slot - 1).wait_send())
        theirs = jnp.dot(other_ref[...], w, preferred_element_type=f32).astype(bf16)
        if s < PACKED:
            for part in range(4):
                wares[s][1][part] = theirs[:, part * TILE:(part + 1) * TILE]
        else:
            wares[s][0][...] = theirs.reshape(8, 80, 4 * TILE)
        pair(s, slot).start()
        pl.when(slot == rings[s].slots - 1)(lambda: pair(s, slot).wait_send())

    def spread(n, rows):
        return lax.dot_general(pick_ref[n], rows, (((0,), (0,)), ((), ())), preferred_element_type=f32).astype(bf16)

    def launch(s, slot):
        ring = rings[s]
        p = lax.rem(slot, 2)
        first_in = ring.ins[0]
        pair(s, slot).wait_recv()
        if s < PACKED:
            own, _, got = wares[s][:3]

            @pl.loop(0, 4)
            def _(part):
                at = pl.multiple_of(part * 1280, 1280)
                first_in[p, pl.ds(at, 640), :] = own[part]
                first_in[p, pl.ds(at + 640, 640), :] = got[p, part]
        else:
            weights = {axis: 4 ** (2 - i) for i, axis in enumerate(ring.axes)}

            @pl.loop(0, 8)
            def _(n):
                rows = spread(n, wares[s][1][p, n])
                for half in range(2):
                    for q in range(4):
                        at = block_at(me, weights, {"z": n // 2, "x": lax.rem(n, 2) * 2 + half, "y": q})
                        first_in[p, pl.ds(at, 128), :] = rows[half * 128:half * 128 + 128, q * TILE:(q + 1) * TILE]
        ring.begin(0, slot)

    def pass_on(s, phase, slot):
        ring = rings[s]
        dst, p = ring.ins[phase + 1], lax.rem(slot, 2)
        if phase == 0 and s < PACKED:
            summed = wares[s][3]

            def hold(at, n, value):
                summed[pl.ds(at, n), :] = value
            ring.finish(0, slot, hold)
            weights = {ring.axes[1]: 4, ring.axes[2]: 1}

            @pl.loop(0, 8)
            def _(n):
                at = pl.multiple_of(n * 80, 16)
                rows = spread(n, jnp.concatenate([summed[pl.ds(at, 80), :], summed[pl.ds(at + 640, 80), :]], axis=0))
                for half in range(2):
                    at = block_at(me, weights, {"z": n // 2, "x": lax.rem(n, 2) * 2 + half})
                    dst[p, pl.ds(at, 128), :] = rows[half * 128:half * 128 + 128]
        else:
            def put(at, n, value):
                dst[p, pl.ds(at, n), :] = value
            ring.finish(phase, slot, put)
        ring.begin(phase + 1, slot)
        ring.close(phase, slot)

    def deliver(s, slot):
        def put(at, n, value):
            out_ref[pl.ds(at, n), pl.ds(tile_of(s, slot), TILE)] = value
        rings[s].finish(2, slot, put)
        rings[s].close(2, slot)

    def stage(step, delay, body, lowest=0):
        for s, (_, _, slots) in enumerate(STREAMS):
            slot = step - delay
            pl.when((slot >= lowest) & (slot < slots))(functools.partial(body, s, slot))

    order = (2, 0, 3, 1)
    start = jnp.int32(0)
    project(order[0], start)
    for before, s in zip(order, order[1:]):
        project(s, start)
        launch(before, start)
    launch(order[-1], start)

    @pl.loop(0, max(slots for _, _, slots in STREAMS) + 6)
    def _(step):
        stage(step, 1, lambda s, slot: rings[s].middle(0, slot))
        stage(step, 3, lambda s, slot: rings[s].middle(1, slot))
        stage(step, 5, lambda s, slot: rings[s].middle(2, slot))
        stage(step, 6, deliver)
        stage(step, 4, lambda s, slot: pass_on(s, 1, slot))
        stage(step, 2, lambda s, slot: pass_on(s, 0, slot))
        stage(step, 0, launch, 1)
        stage(step, -1, project, 1)


def combine(own, other, down, pick):
    quarter = down.shape[1] // 4
    vmem = pl.BlockSpec(memory_space=pltpu.VMEM)
    dma = pltpu.SemaphoreType.DMA
    scratch = [pltpu.SemaphoreType.REGULAR((len(STREAMS), 3, 2))]
    for s in range(len(STREAMS)):
        sizes = (5120 if s < PACKED else 8192, 2048, 512)
        scratch += [rows_buffer(2, n) for n in sizes]
        scratch += [rows_buffer(2, 2, n // 4) for n in sizes]
        scratch += [rows_buffer(2, 2, n // 8) for n in sizes]
        scratch += [dma((3, 4, 2))] * 2
        if s < PACKED:
            scratch += [rows_buffer(4, 640), rows_buffer(4, 640), rows_buffer(2, 4, 640), rows_buffer(1280), dma((1,)), dma((2,))]
        else:
            scratch += [pltpu.VMEM((8, 80, 512), bf16), pltpu.VMEM((2, 8, 160, 512), bf16), dma((1,)), dma((2,))]
    return pl.pallas_call(
        combine_kernel,
        out_shape=jax.ShapeDtypeStruct((128, quarter), bf16),
        in_specs=[vmem] * 4,
        out_specs=vmem,
        scratch_shapes=scratch,
        compiler_params=pltpu.CompilerParams(collective_id=1, has_side_effects=True, vmem_limit_bytes=66900000),
        name="combine",
    )(own, other, down, pick)


def on_device(tokens, routing, gate_codes, w_gate, w_up, w_down):
    codes = jnp.concatenate([routing, gate_codes // 256, gate_codes % 256], axis=1).astype(bf16).T
    meta = jnp.pad(codes, ((0, 32 - codes.shape[0]), (0, 0)))
    own, other, pick = dispatch(tokens, meta, w_gate[0], w_up[0])
    return combine(own, other, w_down[0], pick)


def solution(mesh):
    return jax.shard_map(
        on_device,
        mesh=mesh,
        in_specs=(
            P(("aa", "col"), "ba"),
            P(("aa", "col"), None),
            P(("aa", "col"), None),
            P(("aa", "col"), None, "ba"),
            P(("aa", "col"), None, "ba"),
            P(("aa", "col"), "ba", None),
        ),
        out_specs=P(("aa", "col"), "ba"),
        check_vma=False,
    )
```

time: 550 us -> 272 us (0.49)
  waiting for transfers between devices: 382 us -> 0 us
  Pallas kernels: 0 us -> 268 us
  blocking collectives: 63.4 us -> 0 us
  matrix products: 49 us -> 0 us
  local copies, waits for them, and re-layouts: 19.4 us -> 2.42 us
  between operations: 13.6 us -> 0.02 us
  other arithmetic: 13.4 us -> 1.39 us
  starting transfers between devices: 7.9 us -> 0 us
    pallas_call x0 -> x2, Pallas kernels: none -> 268 us  [the longest x1 137 us: combine(): pl.pallas_call(combine_kernel, out_shape=jax.ShapeDtypeStruct((128, quart...]
    all_gather x1 -> x0, waiting for transfers between devices: 166 us -> none  [on_device(): lax.all_gather(lax.all_to_all(outgoing, ('aa', 'col'), split_axis=0, conc...]
    reduce_scatter x1 -> x0, waiting for transfers between devices: 161 us -> none  [on_device(): lax.psum_scatter(partial_out, 'ba', scatter_dimension=1, tiled=True)]
    all_to_all x1 -> x0, blocking collectives: 63.4 us -> none  [on_device(): lax.all_to_all(outgoing, ('aa', 'col'), split_axis=0, concat_axis=0, tile...]
    all_to_all x1 -> x0, waiting for transfers between devices: 54.6 us -> none  [on_device(): lax.all_to_all(summed.astype(jnp.bfloat16).reshape(sources, count, summed...]
    dot_general x4 -> x0, matrix products: 49 us -> none  [the longest x1 16.7 us: on_device(): gate = jnp.dot(rows, gate_local, preferred_element_type=jnp.float32)]
    gather x2 -> x0, local copies, waits for them, and re-layouts: 16.7 us -> none  [the longest x1 10.9 us: on_device(): table[slot].reshape(tok_rows, top, table.shape[1]).astype(jnp.float32)]
    another operation x3 -> x2, other arithmetic: 9.15 us -> 1.39 us
  transfers between devices with their start and end apart: 3 -> 0, of which waited for: 3 -> 0; matrix products, arithmetic and copies ran while one was open for 0% -> 0% of each run, Pallas kernels for 0% -> 0%
where the time goes in v3:
time: 272 us
  Pallas kernels  268 us (99%)
    pallas_call x1, Pallas kernels, combine(): pl.pallas_call(combine_kernel, out_shape=jax.ShapeDtypeStruct((128, quart...  137 us
    pallas_call x1, Pallas kernels, dispatch(): pl.pallas_call(dispatch_kernel, out_shape=(hidden, hidden, jax.ShapeDtype...  131 us

profile of v3, /device:TPU:0, one launch (start us, length us, event | category | flops | bytes accessed | tf_op | source)
XLA Modules:
  0.0 271.9 jit_solution(11609679949200931918)
XLA Ops:
  0.0 0.7 convert.9
  0.7 0.7 fusion
  1.4 0.6 pad.4.meta_ref
  2.0 131.3 %dispatch.1 = (bf16[640,512]{1,0:T(8,128)(2,1)}, bf16[640,512]{1,0:T(8,128)(2,1)}, bf16[8,160,256]{2,1,0:T(8,128)(2,1)}) custom-call(bf16[128,1792]{1,0:T(8,128)(2,1)} %tok_ref.1, bf16[32,128]{1,0:T(8,128)(2,1)} %pad.4.meta_ref, bf16[7168,512]{1,0:T(8,128)(2,1)} %bitcast.5, bf16[7168,512]{1,0:T(8,128)(2,1)} %bitcast.6), custom_call_target="tpu_custom_call" | custom-call | tf_op jit(solution)/shard_map/dispatch/pallas_call | solution.py:359
  133.3 136.8 %combine.1 = bf16[128,1792]{1,0:T(8,128)(2,1)} custom-call(bf16[640,512]{1,0:T(8,128)(2,1)} %get-tuple-element.8.own_ref, bf16[640,512]{1,0:T(8,128)(2,1)} %get-tuple-element.9.other_ref, bf16[512,7168]{1,0:T(8,128)(2,1)} %bitcast.7, bf16[8,160,256]{2,1,0:T(8,128)(2,1)} %get-tuple-element.10.pick_ref), custom_call_target="tpu_custom_call" | custom-call | tf_op jit(solution)/shard_map/combine/pallas_call | solution.py:582
  270.1 1.8 copy.8
  (1 shorter events, 0.0 us)

commit v4 on v3

--- a/solution.py
+++ b/solution.py
@@ -13,7 +13,7 @@
 TILE = 128
 STREAMS = ((("z", "x", "y"), 0, 4), (("x", "z", "y"), 4, 4), (("y", "z", "x"), 8, 3), (("y", "x", "z"), 11, 3))
 PACKED = 2
-RIGHT, LEFT = 1, -1
+RIGHT, LEFT, ACROSS = 1, -1, 2
 
 
 def place():
@@ -31,20 +31,20 @@
 def greet(me, core):
     barrier = pltpu.get_barrier_semaphore()
     for axis in "xyz":
-        for step in (RIGHT, LEFT):
+        for step in (RIGHT, LEFT, ACROSS):
             pl.semaphore_signal(barrier, inc=1, device_id=peer(me, core, axis, step), device_id_type=MESH)
     pl.semaphore_signal(barrier, inc=1, device_id={"aa": me["z"] * 2 + (1 - core)}, device_id_type=MESH)
-    pl.semaphore_wait(barrier, 7)
-
-
-def grant(me, core, credit, phase, axis):
-    pl.semaphore_signal(credit.at[phase, 0], inc=1, device_id=peer(me, core, axis, RIGHT), device_id_type=MESH)
-    pl.semaphore_signal(credit.at[phase, 1], inc=1, device_id=peer(me, core, axis, LEFT), device_id_type=MESH)
-
-
-def spend(credit, phase):
-    pl.semaphore_wait(credit.at[phase, 0], 1)
-    pl.semaphore_wait(credit.at[phase, 1], 1)
+    pl.semaphore_wait(barrier, 10)
+
+
+def grant(me, core, credit, phase, axis, direct):
+    for i, step in enumerate((RIGHT, LEFT, ACROSS)[:3 if direct else 2]):
+        pl.semaphore_signal(credit.at[phase, i], inc=1, device_id=peer(me, core, axis, step), device_id_type=MESH)
+
+
+def spend(credit, phase, direct):
+    for i in range(3 if direct else 2):
+        pl.semaphore_wait(credit.at[phase, i], 1)
 
 
 def tiles(rows, body):
@@ -90,8 +90,8 @@
 
 
 class Gather:
-    def __init__(self, me, core, axes, outs, sends, recvs, credit, slots):
-        self.me, self.core, self.axes, self.outs = me, core, axes, outs
+    def __init__(self, me, core, axes, direct, outs, sends, recvs, credit, slots):
+        self.me, self.core, self.axes, self.direct, self.outs = me, core, axes, direct, outs
         self.sends, self.recvs, self.credit, self.slots = sends, recvs, credit, slots
 
     def depth(self, phase):
@@ -107,16 +107,17 @@
             (pl.ds(0, b), pl.ds(b, b), LEFT),
             (pl.ds(3 * b, h), pl.ds(2 * b, h), RIGHT),
             (pl.ds(b + h, h), pl.ds(2 * b + h, h), LEFT),
-        )[kind]
+            (pl.ds(0, b), pl.ds(2 * b, b), ACROSS),
+        )[4 if self.direct[phase] and kind == 2 else kind]
         return pltpu.make_async_remote_copy(
             src_ref=buf.at[src], dst_ref=buf.at[dst], send_sem=self.sends[phase].at[kind, p], recv_sem=self.recvs[phase].at[kind, p],
             device_id=peer(self.me, self.core, self.axes[phase], step), device_id_type=MESH)
 
     def begin(self, phase, slot):
         if self.slots > self.depth(phase):
-            pl.when(slot >= self.depth(phase))(lambda: spend(self.credit, phase))
-        self.copy(phase, slot, 0).start()
-        self.copy(phase, slot, 1).start()
+            pl.when(slot >= self.depth(phase))(lambda: spend(self.credit, phase, self.direct[phase]))
+        for kind in range(3 if self.direct[phase] else 2):
+            self.copy(phase, slot, kind).start()
 
     def middle(self, phase, slot):
         self.copy(phase, slot, 0).wait_recv()
@@ -125,15 +126,15 @@
         self.copy(phase, slot, 3).start()
 
     def arrive(self, phase, slot):
-        self.copy(phase, slot, 2).wait_recv()
-        self.copy(phase, slot, 3).wait_recv()
+        for kind in (0, 1, 2) if self.direct[phase] else (2, 3):
+            self.copy(phase, slot, kind).wait_recv()
 
     def close(self, phase, slot):
-        for kind in range(4):
+        for kind in range(3 if self.direct[phase] else 4):
             self.copy(phase, slot, kind).wait_send()
         if self.slots > self.depth(phase):
             pl.when(slot + self.depth(phase) < self.slots)(
-                lambda: grant(self.me, self.core, self.credit, phase, self.axes[phase]))
+                lambda: grant(self.me, self.core, self.credit, phase, self.axes[phase], self.direct[phase]))
 
     def forward(self, phase, slot):
         src, dst = self.outs[phase], self.outs[phase + 1]
@@ -144,7 +145,7 @@
         tiles(src.shape[1], move)
 
 
-def dispatch_kernel(tok_ref, meta_ref, gate_hbm, up_hbm, own_ref, other_ref, pick_ref,
+def dispatch_kernel(tok_ref, routing_ref, codes_ref, gate_hbm, up_hbm, own_ref, other_ref, pick_ref,
                     gate_ref, up_ref, total, gain_own, gain_send, gain_got, gain_sem, load_sem, credit, *rest):
     rest = list(rest)
 
@@ -162,9 +163,9 @@
     greet(me, core)
     rings, wares = [], []
     for s, (axes, _, slots) in enumerate(STREAMS):
-        rings.append(Gather(me, core, axes, take(3), take(3), take(3), credit.at[s], slots))
+        rings.append(Gather(me, core, axes, (True, False, False), take(3), take(3), take(3), credit.at[s], slots))
         wares.append(take(3 if s < PACKED else 5))
-    notes = Gather(me, core, ("x", "z"), take(2), take(2), take(2), None, 1)
+    notes = Gather(me, core, ("x", "z"), (True, True), take(2), take(2), take(2), None, 1)
     gains = pltpu.make_async_remote_copy(
         src_ref=gain_send, dst_ref=gain_got, send_sem=gain_sem.at[0], recv_sem=gain_sem.at[1],
         device_id=partner, device_id_type=MESH)
@@ -198,7 +199,7 @@
         ring.arrive(phase, slot)
         if phase == 1 and s < PACKED:
             src, dst = ring.outs[1], ring.outs[2]
-            p, q = lax.rem(slot, 2), lax.rem(slot, ring.depth(2))
+            p, q = lax.rem(slot, ring.depth(1)), lax.rem(slot, ring.depth(2))
             weights = {ring.axes[0]: 1, ring.axes[1]: 4}
 
             @pl.loop(0, 8)
@@ -286,7 +287,11 @@
         pl.when(step == at)(body)
 
     def note_open():
-        notes.outs[0][0, 0:32, :] = meta_ref[...]
+        nothing = jnp.zeros((128, 112), f32)
+        both = jnp.concatenate([routing_ref[...].astype(f32), codes_ref[...].astype(f32), nothing], axis=1).T
+        high = jnp.floor(both[8:16] * (1.0 / 256.0))
+        notes.outs[0][0, 0:32, :] = jnp.concatenate(
+            [both[0:8], high, both[8:16] - 256.0 * high, both[16:24]], axis=0).astype(bf16)
         notes.begin(0, 0)
 
     def note_pass():
@@ -300,28 +305,36 @@
         tables()
         notes.close(1, 0)
 
-    @pl.loop(0, max(slots for _, _, slots in STREAMS) + 6)
+    def consume(step):
+        def one(s, body):
+            slot = step - 5
+            pl.when((slot >= 0) & (slot < STREAMS[s][2]))(lambda: body(s, slot))
+
+        for s in (2, 3, 0):
+            one(s, collect)
+        for s in (2, 3, 0):
+            one(s, multiply)
+        one(1, collect)
+        one(1, multiply)
+
+    @pl.loop(0, max(slots for _, _, slots in STREAMS) + 5)
     def _(step):
-        note(step, 4, note_end)
-        note(step, 3, lambda: notes.middle(1, 0))
-        note(step, 2, note_pass)
-        note(step, 1, lambda: notes.middle(0, 0))
+        note(step, 2, note_end)
+        note(step, 1, note_pass)
         note(step, 0, note_open)
-        stage(step, 5, lambda s, slot: rings[s].middle(2, slot))
-        stage(step, 4, lambda s, slot: pass_on(s, 1, slot))
-        stage(step, 3, lambda s, slot: rings[s].middle(1, slot))
-        stage(step, 2, lambda s, slot: pass_on(s, 0, slot))
-        stage(step, 1, lambda s, slot: rings[s].middle(0, slot))
+        stage(step, 2, lambda s, slot: rings[s].middle(1, slot))
+        stage(step, 1, lambda s, slot: pass_on(s, 0, slot))
         stage(step, 0, open_tile)
-        stage(step, 6, collect)
-
-        @pl.when(step == 5)
+        stage(step, 4, lambda s, slot: rings[s].middle(2, slot))
+        stage(step, 3, lambda s, slot: pass_on(s, 1, slot))
+
+        @pl.when(step == 4)
         def _():
             total[...] = jnp.zeros_like(total)
             for load in loads:
                 load.wait()
 
-        stage(step, 6, multiply)
+        consume(step)
 
     gains.wait()
 
@@ -338,7 +351,7 @@
     return pltpu.VMEM(shape + (TILE,), bf16)
 
 
-def dispatch(tokens, meta, gate, up):
+def dispatch(tokens, routing, codes, gate, up):
     vmem = pl.BlockSpec(memory_space=pltpu.VMEM)
     hbm = pl.BlockSpec(memory_space=pl.ANY)
     dma = pltpu.SemaphoreType.DMA
@@ -346,11 +359,11 @@
     scratch = [
         pltpu.VMEM(gate.shape, bf16), pltpu.VMEM(up.shape, bf16), pltpu.VMEM((2, 640, 1024), f32),
         pltpu.VMEM((8, 80, 128), f32), pltpu.VMEM((8, 80, 128), f32), pltpu.VMEM((8, 80, 128), f32),
-        dma((2,)), dma((2,)), pltpu.SemaphoreType.REGULAR((len(STREAMS), 3, 2)),
+        dma((2,)), dma((2,)), pltpu.SemaphoreType.REGULAR((len(STREAMS), 3, 3)),
     ]
     for s in range(len(STREAMS)):
-        scratch += [rows_buffer(2, 512), rows_buffer(2, 2048), rows_buffer(3, 5120 if s < PACKED else 8192)]
-        scratch += [dma((4, 2)), dma((4, 2)), dma((4, 3))] * 2
+        scratch += [rows_buffer(2, 512), rows_buffer(3, 2048), rows_buffer(3, 5120 if s < PACKED else 8192)]
+        scratch += [dma((4, 2)), dma((4, 3)), dma((4, 3))] * 2
         if s < PACKED:
             scratch += [rows_buffer(2, 4, 640), dma((4,)), dma((2, 4))]
         else:
@@ -359,43 +372,54 @@
     return pl.pallas_call(
         dispatch_kernel,
         out_shape=(hidden, hidden, jax.ShapeDtypeStruct((8, 160, 256), bf16)),
-        in_specs=[vmem, vmem, hbm, hbm],
+        in_specs=[vmem, vmem, vmem, hbm, hbm],
         out_specs=(vmem,) * 3,
         scratch_shapes=scratch,
         compiler_params=pltpu.CompilerParams(collective_id=0, has_side_effects=True, vmem_limit_bytes=66900000),
         name="dispatch",
-    )(tokens, meta, gate, up)
+    )(tokens, routing, codes, gate, up)
 
 
 class Reduce:
-    def __init__(self, me, core, axes, ins, gots, mores, sends, recvs, credit, slots):
-        self.me, self.core, self.axes = me, core, axes
+    def __init__(self, me, core, axes, direct, ins, gots, mores, sends, recvs, credit, slots):
+        self.me, self.core, self.axes, self.direct = me, core, axes, direct
         self.ins, self.gots, self.mores = ins, gots, mores
         self.sends, self.recvs, self.credit, self.slots = sends, recvs, credit, slots
 
+    def depth(self, phase):
+        return self.ins[phase].shape[0]
+
     def copy(self, phase, slot, kind):
-        p = lax.rem(slot, 2)
+        p = lax.rem(slot, self.depth(phase))
         buf = self.ins[phase].at[p]
         b = self.ins[phase].shape[1] // 4
         h = b // 2
         got, more = self.gots[phase], self.mores[phase]
-        src, dst, step = (
-            (pl.ds(b + h, b), got.at[p, 0], RIGHT),
-            (pl.ds(2 * b + h, b), got.at[p, 1], LEFT),
-            (pl.ds(b, h), more.at[p, 0], RIGHT),
-            (pl.ds(3 * b + h, h), more.at[p, 1], LEFT),
-        )[kind]
+        if self.direct[phase]:
+            src, dst, step = (
+                (pl.ds(b, b), got.at[p, 0], RIGHT),
+                (pl.ds(3 * b, b), got.at[p, 1], LEFT),
+                (pl.ds(2 * b, b), more.at[p, 0], ACROSS),
+            )[kind]
+        else:
+            src, dst, step = (
+                (pl.ds(b + h, b), got.at[p, 0], RIGHT),
+                (pl.ds(2 * b + h, b), got.at[p, 1], LEFT),
+                (pl.ds(b, h), more.at[p, 0], RIGHT),
+                (pl.ds(3 * b + h, h), more.at[p, 1], LEFT),
+            )[kind]
         return pltpu.make_async_remote_copy(
-            src_ref=buf.at[src], dst_ref=dst, send_sem=self.sends.at[phase, kind, p], recv_sem=self.recvs.at[phase, kind, p],
+            src_ref=buf.at[src], dst_ref=dst, send_sem=self.sends[phase].at[kind, p], recv_sem=self.recvs[phase].at[kind, p],
             device_id=peer(self.me, self.core, self.axes[phase], step), device_id_type=MESH)
 
     def begin(self, phase, slot):
-        pl.when(slot >= 2)(lambda: spend(self.credit, phase))
-        self.copy(phase, slot, 0).start()
-        self.copy(phase, slot, 1).start()
+        if self.slots > self.depth(phase):
+            pl.when(slot >= self.depth(phase))(lambda: spend(self.credit, phase, self.direct[phase]))
+        for kind in range(3 if self.direct[phase] else 2):
+            self.copy(phase, slot, kind).start()
 
     def middle(self, phase, slot):
-        p = lax.rem(slot, 2)
+        p = lax.rem(slot, self.depth(phase))
         buf, got = self.ins[phase], self.gots[phase]
         b = buf.shape[1] // 4
         h = b // 2
@@ -409,10 +433,20 @@
             self.copy(phase, slot, kind + 2).start()
 
     def finish(self, phase, slot, put):
-        p = lax.rem(slot, 2)
+        p = lax.rem(slot, self.depth(phase))
         buf, got, more = self.ins[phase], self.gots[phase], self.mores[phase]
         b = buf.shape[1] // 4
         h = b // 2
+        if self.direct[phase]:
+            for kind in range(3):
+                self.copy(phase, slot, kind).wait_recv()
+
+            def add_all(at, n):
+                value = ((buf[p, pl.ds(at, n), :].astype(f32) + got[p, 0, pl.ds(at, n), :].astype(f32))
+                         + (got[p, 1, pl.ds(at, n), :].astype(f32) + more[p, 0, pl.ds(at, n), :].astype(f32)))
+                put(at, n, value.astype(bf16))
+            tiles(b, add_all)
+            return
         for kind, base, skip in ((0, 0, h), (1, h, 0)):
             self.copy(phase, slot, kind + 2).wait_recv()
 
@@ -424,12 +458,14 @@
             tiles(h, add)
 
     def close(self, phase, slot):
-        for kind in range(4):
+        for kind in range(3 if self.direct[phase] else 4):
             self.copy(phase, slot, kind).wait_send()
-        pl.when(slot + 2 < self.slots)(lambda: grant(self.me, self.core, self.credit, phase, self.axes[phase]))
-
-
-def combine_kernel(own_ref, other_ref, down_ref, pick_ref, out_ref, credit, *rest):
+        if self.slots > self.depth(phase):
+            pl.when(slot + self.depth(phase) < self.slots)(
+                lambda: grant(self.me, self.core, self.credit, phase, self.axes[phase], self.direct[phase]))
+
+
+def combine_kernel(own_ref, other_ref, down_hbm, pick_ref, out_ref, down_ref, load_sem, credit, *rest):
     rest = list(rest)
 
     def take(n):
@@ -440,10 +476,24 @@
     me, core = place()
     partner = {"aa": me["z"] * 2 + (1 - core)}
     quarter = out_ref.shape[1]
+    order = (0, 2, 1, 3)
+
+    def load(s, slot, part):
+        q = lax.rem(me["y"] + part, 4) if s < PACKED else part
+        at = slot + STREAMS[s][1]
+        return pltpu.make_async_copy(
+            down_hbm.at[:, pl.ds(pl.multiple_of(q * quarter + at * TILE, TILE), TILE)],
+            down_ref.at[at, :, pl.ds(part * TILE, TILE)], load_sem.at[at, part])
+
+    for slot in range(max(slots for _, _, slots in STREAMS)):
+        for s in order:
+            if slot < STREAMS[s][2]:
+                for part in range(4):
+                    load(s, slot, part).start()
     greet(me, core)
     rings, wares = [], []
     for s, (axes, _, slots) in enumerate(STREAMS):
-        rings.append(Reduce(me, core, axes[::-1], take(3), take(3), take(3), *take(2), credit.at[s], slots))
+        rings.append(Reduce(me, core, axes[::-1], (False, False, True), take(3), take(3), take(3), take(3), take(3), credit.at[s], slots))
         wares.append(take(6 if s < PACKED else 4))
 
     def pair(s, slot):
@@ -461,9 +511,9 @@
         return pl.multiple_of((slot + STREAMS[s][1]) * TILE, TILE)
 
     def project(s, slot):
-        first = tile_of(s, slot)
-        quarters = [lax.rem(me["y"] + part, 4) for part in range(4)] if s < PACKED else range(4)
-        w = jnp.concatenate([down_ref[:, pl.ds(pl.multiple_of(q * quarter + first, TILE), TILE)] for q in quarters], axis=1)
+        for part in range(4):
+            load(s, slot, part).wait()
+        w = down_ref[slot + STREAMS[s][1]]
         mine = jnp.dot(own_ref[...], w, preferred_element_type=f32).astype(bf16)
         if s < PACKED:
             for part in range(4):
@@ -485,7 +535,7 @@
 
     def launch(s, slot):
         ring = rings[s]
-        p = lax.rem(slot, 2)
+        p, d = lax.rem(slot, ring.depth(0)), lax.rem(slot, 2)
         first_in = ring.ins[0]
         pair(s, slot).wait_recv()
         if s < PACKED:
@@ -495,13 +545,13 @@
             def _(part):
                 at = pl.multiple_of(part * 1280, 1280)
                 first_in[p, pl.ds(at, 640), :] = own[part]
-                first_in[p, pl.ds(at + 640, 640), :] = got[p, part]
+                first_in[p, pl.ds(at + 640, 640), :] = got[d, part]
         else:
             weights = {axis: 4 ** (2 - i) for i, axis in enumerate(ring.axes)}
 
             @pl.loop(0, 8)
             def _(n):
-                rows = spread(n, wares[s][1][p, n])
+                rows = spread(n, wares[s][1][d, n])
                 for half in range(2):
                     for q in range(4):
                         at = block_at(me, weights, {"z": n // 2, "x": lax.rem(n, 2) * 2 + half, "y": q})
@@ -539,28 +589,30 @@
         rings[s].finish(2, slot, put)
         rings[s].close(2, slot)
 
-    def stage(step, delay, body, lowest=0):
-        for s, (_, _, slots) in enumerate(STREAMS):
+    def stage(step, delay, body, lowest=0, streams=range(len(STREAMS))):
+        for s in streams:
             slot = step - delay
-            pl.when((slot >= lowest) & (slot < slots))(functools.partial(body, s, slot))
-
-    order = (2, 0, 3, 1)
+            pl.when((slot >= lowest) & (slot < STREAMS[s][2]))(functools.partial(body, s, slot))
+
     start = jnp.int32(0)
     project(order[0], start)
     for before, s in zip(order, order[1:]):
         project(s, start)
         launch(before, start)
     launch(order[-1], start)
-
-    @pl.loop(0, max(slots for _, _, slots in STREAMS) + 6)
+    packed, plain = range(PACKED), range(PACKED, len(STREAMS))
+
+    @pl.loop(0, max(slots for _, _, slots in STREAMS) + 5)
     def _(step):
         stage(step, 1, lambda s, slot: rings[s].middle(0, slot))
+        stage(step, 0, launch, 1, packed)
         stage(step, 3, lambda s, slot: rings[s].middle(1, slot))
-        stage(step, 5, lambda s, slot: rings[s].middle(2, slot))
-        stage(step, 6, deliver)
+        stage(step, 5, deliver)
         stage(step, 4, lambda s, slot: pass_on(s, 1, slot))
-        stage(step, 2, lambda s, slot: pass_on(s, 0, slot))
-        stage(step, 0, launch, 1)
+        for s in plain:
+            stage(step, 2, lambda s, slot: pass_on(s, 0, slot), 0, (s,))
+            stage(step, 0, launch, 1, (s,))
+        stage(step, 2, lambda s, slot: pass_on(s, 0, slot), 0, packed)
         stage(step, -1, project, 1)
 
 
@@ -568,13 +620,15 @@
     quarter = down.shape[1] // 4
     vmem = pl.BlockSpec(memory_space=pltpu.VMEM)
     dma = pltpu.SemaphoreType.DMA
-    scratch = [pltpu.SemaphoreType.REGULAR((len(STREAMS), 3, 2))]
+    count = quarter // TILE
+    scratch = [pltpu.VMEM((count, down.shape[0], 4 * TILE), bf16), dma((count, 4)), pltpu.SemaphoreType.REGULAR((len(STREAMS), 3, 3))]
     for s in range(len(STREAMS)):
         sizes = (5120 if s < PACKED else 8192, 2048, 512)
-        scratch += [rows_buffer(2, n) for n in sizes]
-        scratch += [rows_buffer(2, 2, n // 4) for n in sizes]
-        scratch += [rows_buffer(2, 2, n // 8) for n in sizes]
-        scratch += [dma((3, 4, 2))] * 2
+        depths = (3 if s < PACKED else 2, 2, 2)
+        scratch += [rows_buffer(d, n) for d, n in zip(depths, sizes)]
+        scratch += [rows_buffer(d, 2, n // 4) for d, n in zip(depths, sizes)]
+        scratch += [rows_buffer(depths[0], 2, sizes[0] // 8), rows_buffer(2, 2, sizes[1] // 8), rows_buffer(2, 1, sizes[2] // 4)]
+        scratch += [dma((4, d)) for d in depths] * 2
         if s < PACKED:
             scratch += [rows_buffer(4, 640), rows_buffer(4, 640), rows_buffer(2, 4, 640), rows_buffer(1280), dma((1,)), dma((2,))]
         else:
@@ -582,7 +636,7 @@
     return pl.pallas_call(
         combine_kernel,
         out_shape=jax.ShapeDtypeStruct((128, quarter), bf16),
-        in_specs=[vmem] * 4,
+        in_specs=[vmem, vmem, pl.BlockSpec(memory_space=pl.ANY), vmem],
         out_specs=vmem,
         scratch_shapes=scratch,
         compiler_params=pltpu.CompilerParams(collective_id=1, has_side_effects=True, vmem_limit_bytes=66900000),
@@ -591,9 +645,7 @@
 
 
 def on_device(tokens, routing, gate_codes, w_gate, w_up, w_down):
-    codes = jnp.concatenate([routing, gate_codes // 256, gate_codes % 256], axis=1).astype(bf16).T
-    meta = jnp.pad(codes, ((0, 32 - codes.shape[0]), (0, 0)))
-    own, other, pick = dispatch(tokens, meta, w_gate[0], w_up[0])
+    own, other, pick = dispatch(tokens, routing, gate_codes, w_gate[0], w_up[0])
     return combine(own, other, w_down[0], pick)
 
 

time: 272 us -> 269 us (0.989)
  Pallas kernels: 268 us -> 264 us
    pallas_call x1, Pallas kernels: 137 us -> 122 us  [combine(): pl.pallas_call(combine_kernel, out_shape=jax.ShapeDtypeStruct((128, quart...]
    pallas_call x1, Pallas kernels: 131 us -> 142 us  [dispatch(): pl.pallas_call(dispatch_kernel, out_shape=(hidden, hidden, jax.ShapeDtype...]
    unnamed x1 -> x3, local copies, waits for them, and re-layouts: 1.82 us -> 4.64 us
where the time goes in v4:
time: 269 us; the launch traced here: 268 us
  Pallas kernels  264 us (98%)
  local copies, waits for them, and re-layouts  4.64 us (2%)
    pallas_call x1, Pallas kernels, dispatch(): pl.pallas_call(dispatch_kernel, out_shape=(hidden, hidden, jax.ShapeDtype...  142 us
    pallas_call x1, Pallas kernels, combine(): pl.pallas_call(combine_kernel, out_shape=jax.ShapeDtypeStruct((128, quart...  122 us

profile of v4, /device:TPU:0, one launch (start us, length us, event | category | flops | bytes accessed | tf_op | source)
XLA Modules:
  0.0 268.4 jit_solution(12403255391441377672)
XLA Ops:
  0.0 1.4 copy.7.routing_ref
  1.4 1.4 copy.8.codes_ref
  2.8 141.9 %dispatch.1 = (bf16[640,512]{1,0:T(8,128)(2,1)}, bf16[640,512]{1,0:T(8,128)(2,1)}, bf16[8,160,256]{2,1,0:T(8,128)(2,1)}) custom-call(bf16[128,1792]{1,0:T(8,128)(2,1)} %tok_ref.1, s32[128,8]{1,0:T(8,128)} %copy.7.routing_ref, s32[128,8]{1,0:T(8,128)} %copy.8.codes_ref, bf16[7168,512]{1,0:T(8,128)(2,1)} %bitcast.4, bf16[7168,512]{1,0:T(8,128)(2,1)} %bitcast.5), custom_call_target="tpu_custom_call" | custom-call | tf_op jit(solution)/shard_map/dispatch/pallas_call | solution.py:372
  144.7 121.9 %combine.1 = bf16[128,1792]{1,0:T(8,128)(2,1)} custom-call(bf16[640,512]{1,0:T(8,128)(2,1)} %get-tuple-element.8.own_ref, bf16[640,512]{1,0:T(8,128)(2,1)} %get-tuple-element.9.other_ref, bf16[512,7168]{1,0:T(8,128)(2,1)} %bitcast.3, bf16[8,160,256]{2,1,0:T(8,128)(2,1)} %get-tuple-element.10.pick_ref), custom_call_target="tpu_custom_call" | custom-call | tf_op jit(solution)/shard_map/combine/pallas_call | solution.py:636
  266.6 1.8 copy.10

commit v5 on v4

--- a/solution.py
+++ b/solution.py
@@ -34,7 +34,10 @@
         for step in (RIGHT, LEFT, ACROSS):
             pl.semaphore_signal(barrier, inc=1, device_id=peer(me, core, axis, step), device_id_type=MESH)
     pl.semaphore_signal(barrier, inc=1, device_id={"aa": me["z"] * 2 + (1 - core)}, device_id_type=MESH)
-    pl.semaphore_wait(barrier, 10)
+
+
+def meet():
+    pl.semaphore_wait(pltpu.get_barrier_semaphore(), 10)
 
 
 def grant(me, core, credit, phase, axis, direct):
@@ -158,9 +161,10 @@
     partner = {"aa": me["z"] * 2 + (1 - core)}
     quarter = tok_ref.shape[1]
     loads = [pltpu.make_async_copy(gate_hbm, gate_ref, load_sem.at[0]), pltpu.make_async_copy(up_hbm, up_ref, load_sem.at[1])]
+    greet(me, core)
     for load in loads:
         load.start()
-    greet(me, core)
+    meet()
     rings, wares = [], []
     for s, (axes, _, slots) in enumerate(STREAMS):
         rings.append(Gather(me, core, axes, (True, False, False), take(3), take(3), take(3), credit.at[s], slots))
@@ -287,11 +291,10 @@
         pl.when(step == at)(body)
 
     def note_open():
-        nothing = jnp.zeros((128, 112), f32)
-        both = jnp.concatenate([routing_ref[...].astype(f32), codes_ref[...].astype(f32), nothing], axis=1).T
-        high = jnp.floor(both[8:16] * (1.0 / 256.0))
+        codes = codes_ref[...].astype(f32)
+        high = jnp.floor(codes * (1.0 / 256.0))
         notes.outs[0][0, 0:32, :] = jnp.concatenate(
-            [both[0:8], high, both[8:16] - 256.0 * high, both[16:24]], axis=0).astype(bf16)
+            [routing_ref[...].astype(f32), high, codes - 256.0 * high, jnp.zeros((8, 128), f32)], axis=0).astype(bf16)
         notes.begin(0, 0)
 
     def note_pass():
@@ -310,27 +313,28 @@
             slot = step - 5
             pl.when((slot >= 0) & (slot < STREAMS[s][2]))(lambda: body(s, slot))
 
-        for s in (2, 3, 0):
+        for s in range(len(STREAMS)):
             one(s, collect)
-        for s in (2, 3, 0):
+        for s in range(len(STREAMS)):
             one(s, multiply)
-        one(1, collect)
-        one(1, multiply)
 
     @pl.loop(0, max(slots for _, _, slots in STREAMS) + 5)
     def _(step):
-        note(step, 2, note_end)
         note(step, 1, note_pass)
         note(step, 0, note_open)
+        stage(step, 4, lambda s, slot: rings[s].middle(2, slot))
+        stage(step, 3, lambda s, slot: pass_on(s, 1, slot))
         stage(step, 2, lambda s, slot: rings[s].middle(1, slot))
         stage(step, 1, lambda s, slot: pass_on(s, 0, slot))
         stage(step, 0, open_tile)
-        stage(step, 4, lambda s, slot: rings[s].middle(2, slot))
-        stage(step, 3, lambda s, slot: pass_on(s, 1, slot))
+        note(step, 2, note_end)
+
+        @pl.when(step == 1)
+        def _():
+            total[...] = jnp.zeros_like(total)
 
         @pl.when(step == 4)
         def _():
-            total[...] = jnp.zeros_like(total)
             for load in loads:
                 load.wait()
 
@@ -476,7 +480,7 @@
     me, core = place()
     partner = {"aa": me["z"] * 2 + (1 - core)}
     quarter = out_ref.shape[1]
-    order = (0, 2, 1, 3)
+    order = (0, 1, 2, 3)
 
     def load(s, slot, part):
         q = lax.rem(me["y"] + part, 4) if s < PACKED else part
@@ -485,12 +489,13 @@
             down_hbm.at[:, pl.ds(pl.multiple_of(q * quarter + at * TILE, TILE), TILE)],
             down_ref.at[at, :, pl.ds(part * TILE, TILE)], load_sem.at[at, part])
 
+    greet(me, core)
     for slot in range(max(slots for _, _, slots in STREAMS)):
         for s in order:
             if slot < STREAMS[s][2]:
                 for part in range(4):
                     load(s, slot, part).start()
-    greet(me, core)
+    meet()
     rings, wares = [], []
     for s, (axes, _, slots) in enumerate(STREAMS):
         rings.append(Reduce(me, core, axes[::-1], (False, False, True), take(3), take(3), take(3), take(3), take(3), credit.at[s], slots))
@@ -645,7 +650,7 @@
 
 
 def on_device(tokens, routing, gate_codes, w_gate, w_up, w_down):
-    own, other, pick = dispatch(tokens, routing, gate_codes, w_gate[0], w_up[0])
+    own, other, pick = dispatch(tokens, routing.T, gate_codes.T, w_gate[0], w_up[0])
     return combine(own, other, w_down[0], pick)
 
 

time: 269 us -> 256 us (0.952)
  Pallas kernels: 264 us -> 254 us
  local copies, waits for them, and re-layouts: 4.64 us -> 1.82 us
    pallas_call x1, Pallas kernels: 142 us -> 131 us  [dispatch(): pl.pallas_call(dispatch_kernel, out_shape=(hidden, hidden, jax.ShapeDtype...]
    unnamed x3 -> x1, local copies, waits for them, and re-layouts: 4.64 us -> 1.82 us
where the time goes in v5:
time: 256 us
  Pallas kernels  254 us (99%)
    pallas_call x1, Pallas kernels, dispatch(): pl.pallas_call(dispatch_kernel, out_shape=(hidden, hidden, jax.ShapeDtype...  131 us
    pallas_call x1, Pallas kernels, combine(): pl.pallas_call(combine_kernel, out_shape=jax.ShapeDtypeStruct((128, quart...  123 us

profile of v5, /device:TPU:0, one launch (start us, length us, event | category | flops | bytes accessed | tf_op | source)
XLA Modules:
  0.0 255.7 jit_solution(9808146530530236826)
XLA Ops:
  0.0 131.2 %dispatch.1 = (bf16[640,512]{1,0:T(8,128)(2,1)}, bf16[640,512]{1,0:T(8,128)(2,1)}, bf16[8,160,256]{2,1,0:T(8,128)(2,1)}) custom-call(bf16[128,1792]{1,0:T(8,128)(2,1)} %tok_ref.1, s32[8,128]{1,0:T(8,128)} %bitcast.8, s32[8,128]{1,0:T(8,128)} %bitcast.9, bf16[7168,512]{1,0:T(8,128)(2,1)} %bitcast.5, bf16[7168,512]{1,0:T(8,128)(2,1)} %bitcast.6), custom_call_target="tpu_custom_call" | custom-call | tf_op jit(solution)/shard_map/dispatch/pallas_call | solution.py:376
  131.3 122.7 %combine.1 = bf16[128,1792]{1,0:T(8,128)(2,1)} custom-call(bf16[640,512]{1,0:T(8,128)(2,1)} %get-tuple-element.8.own_ref, bf16[640,512]{1,0:T(8,128)(2,1)} %get-tuple-element.9.other_ref, bf16[512,7168]{1,0:T(8,128)(2,1)} %bitcast.7, bf16[8,160,256]{2,1,0:T(8,128)(2,1)} %get-tuple-element.10.pick_ref), custom_call_target="tpu_custom_call" | custom-call | tf_op jit(solution)/shard_map/combine/pallas_call | solution.py:641
  253.9 1.8 copy.8

commit v6 on v5

--- a/solution.py
+++ b/solution.py
@@ -448,7 +448,7 @@
             def add_all(at, n):
                 value = ((buf[p, pl.ds(at, n), :].astype(f32) + got[p, 0, pl.ds(at, n), :].astype(f32))
                          + (got[p, 1, pl.ds(at, n), :].astype(f32) + more[p, 0, pl.ds(at, n), :].astype(f32)))
-                put(at, n, value.astype(bf16))
+                put(at, n, value)
             tiles(b, add_all)
             return
         for kind, base, skip in ((0, 0, h), (1, h, 0)):
@@ -640,7 +640,7 @@
             scratch += [pltpu.VMEM((8, 80, 512), bf16), pltpu.VMEM((2, 8, 160, 512), bf16), dma((1,)), dma((2,))]
     return pl.pallas_call(
         combine_kernel,
-        out_shape=jax.ShapeDtypeStruct((128, quarter), bf16),
+        out_shape=jax.ShapeDtypeStruct((128, quarter), f32),
         in_specs=[vmem, vmem, pl.BlockSpec(memory_space=pl.ANY), vmem],
         out_specs=vmem,
         scratch_shapes=scratch,
@@ -651,7 +651,7 @@
 
 def on_device(tokens, routing, gate_codes, w_gate, w_up, w_down):
     own, other, pick = dispatch(tokens, routing.T, gate_codes.T, w_gate[0], w_up[0])
-    return combine(own, other, w_down[0], pick)
+    return combine(own, other, w_down[0], pick).astype(bf16)
 
 
 def solution(mesh):

time: 256 us -> 256 us (level)
  no operation moved by 1% of the time
where the time goes in v6:
time: 256 us
  Pallas kernels  254 us (99%)
    pallas_call x1, Pallas kernels, dispatch(): pl.pallas_call(dispatch_kernel, out_shape=(hidden, hidden, jax.ShapeDtype...  131 us
    pallas_call x1, Pallas kernels, combine(): pl.pallas_call(combine_kernel, out_shape=jax.ShapeDtypeStruct((128, quart...  123 us

profile of v6, /device:TPU:0, one launch (start us, length us, event | category | flops | bytes accessed | tf_op | source)
XLA Modules:
  0.0 256.1 jit_solution(1651113455457493819)
XLA Ops:
  0.0 131.3 %dispatch.1 = (bf16[640,512]{1,0:T(8,128)(2,1)}, bf16[640,512]{1,0:T(8,128)(2,1)}, bf16[8,160,256]{2,1,0:T(8,128)(2,1)}) custom-call(bf16[128,1792]{1,0:T(8,128)(2,1)} %tok_ref.1, s32[8,128]{1,0:T(8,128)} %bitcast.8, s32[8,128]{1,0:T(8,128)} %bitcast.9, bf16[7168,512]{1,0:T(8,128)(2,1)} %bitcast.5, bf16[7168,512]{1,0:T(8,128)(2,1)} %bitcast.6), custom_call_target="tpu_custom_call" | custom-call | tf_op jit(solution)/shard_map/dispatch/pallas_call | solution.py:376
  131.3 122.8 %combine.1 = f32[128,1792]{1,0:T(8,128)} custom-call(bf16[640,512]{1,0:T(8,128)(2,1)} %get-tuple-element.8.own_ref, bf16[640,512]{1,0:T(8,128)(2,1)} %get-tuple-element.9.other_ref, bf16[512,7168]{1,0:T(8,128)(2,1)} %bitcast.7, bf16[8,160,256]{2,1,0:T(8,128)(2,1)} %get-tuple-element.10.pick_ref), custom_call_target="tpu_custom_call" | custom-call | tf_op jit(solution)/shard_map/combine/pallas_call | solution.py:641
  254.1 2.0 convert_element_type.3
